TPU v7x, 8 devices: a whole 2x2x1 slice. The times are simulated.
8 devices in a mesh: my: 4 (over z, y, x), mx: 2 (over core).
Axes of the slice: x: 2, y: 2, z: 1, core: 2. Of those that a mesh axis runs over, the one named last changes fastest.
Arguments:
- x_in: bfloat16 [256, 5120], P(None, 'mx')
- seq_lens: int32 [256], P('mx')
- gain_attn: bfloat16 [5120], P('mx')
- gain_mlp: bfloat16 [5120], P('mx')
- w_q: bfloat16 [5120, 5120], P('mx', 'my')
- b_q: bfloat16 [5120], P('my')
- w_k: bfloat16 [5120, 1024], P('mx', 'my')
- b_k: bfloat16 [1024], P('my')
- w_v: bfloat16 [5120, 1024], P('mx', 'my')
- b_v: bfloat16 [1024], P('my')
- w_o: bfloat16 [5120, 5120], P('my', 'mx')
- w_gate: bfloat16 [5120, 27392], P('mx', 'my')
- w_up: bfloat16 [5120, 27392], P('mx', 'my')
- w_down: bfloat16 [27392, 5120], P('my', 'mx')
- k_cache: bfloat16 [256, 256, 8, 128], P('mx', None, 'my')
- v_cache: bfloat16 [256, 256, 8, 128], P('mx', None, 'my')
Outputs:
- output 1: bfloat16 [256, 5120], P(None, 'mx')
- output 2: bfloat16 [256, 256, 8, 128], P('mx', None, 'my')
- output 3: bfloat16 [256, 256, 8, 128], P('mx', None, 'my')
All inputs are finite; a program needn't handle non-finite values.
Results may differ from a plain program's by a relative error of at most 0.0165306.
Values are sent between devices in bfloat16 or wider.
A program may use at most 1 GiB of HBM per device.

v0:
```python
import jax
import jax.numpy as jnp
from jax import lax
from jax.sharding import PartitionSpec as P

HEAD = 128
NORM_EPS = 1e-6
ROPE_THETA = 1000000.0


def apply_rotary(vectors, positions):
    half_dim = HEAD // 2
    inv_freq = ROPE_THETA ** (-2.0 * jnp.arange(half_dim, dtype=jnp.float32) / HEAD)
    angles = positions.astype(jnp.float32)[:, None, None] * inv_freq
    cos_tab = jnp.cos(angles)
    sin_tab = jnp.sin(angles)
    lower_half = vectors[..., :half_dim]
    upper_half = vectors[..., half_dim:]
    return jnp.concatenate([lower_half * cos_tab - upper_half * sin_tab, upper_half * cos_tab + lower_half * sin_tab], axis=-1)


def attend_local(q_rot, k_cache_out, v_cache_out, seq_lens):
    row_count, seq_len, kv_heads, _ = k_cache_out.shape
    q_heads = q_rot.shape[1]
    q_grouped = q_rot.reshape(row_count, kv_heads, q_heads // kv_heads, HEAD)
    scores = jnp.einsum("bkgd,bskd->bkgs", q_grouped, k_cache_out, preferred_element_type=jnp.float32) * HEAD ** -0.5
    visible = (jnp.arange(seq_len)[None, :] <= seq_lens[:, None])[:, None, None, :]
    scores = jnp.where(visible, scores, -jnp.inf)
    weights = jnp.exp(scores - jnp.max(scores, axis=-1, keepdims=True))
    weight_sum = jnp.sum(weights, axis=-1, keepdims=True)
    weighted = jnp.einsum("bkgs,bskd->bkgd", weights.astype(jnp.bfloat16), v_cache_out, preferred_element_type=jnp.float32)
    return (weighted / weight_sum).astype(jnp.bfloat16).reshape(row_count, q_heads * HEAD)


def solution(mesh):
    mx_size = mesh.shape["mx"]
    act_spec = P(None, "mx")
    cache_spec = P("mx", None, "my", None)
    in_specs = (act_spec, P("mx"), P("mx"), P("mx"), P("mx", "my"), P("my"), P("mx", "my"), P("my"), P("mx", "my"), P("my"), P("my", "mx"), P("mx", "my"), P("mx", "my"), P("my", "mx"), cache_spec, cache_spec)
    out_specs = (act_spec, cache_spec, cache_spec)

    def local_layer(x_in, seq_lens, gain_attn, gain_mlp, w_q, b_q, w_k, b_k, w_v, b_v, w_o, w_gate, w_up, w_down, k_cache, v_cache):
        hidden = x_in.shape[1] * mx_size
        x_f32 = x_in.astype(jnp.float32)
        attn_sq = lax.psum(jnp.sum(x_f32 * x_f32, axis=1, keepdims=True), "mx")
        normed = (x_f32 * lax.rsqrt(attn_sq / hidden + NORM_EPS) * gain_attn.astype(jnp.float32)).astype(jnp.bfloat16)
        q_cols = w_q.shape[1]
        kv_cols = w_k.shape[1]
        partials = jnp.concatenate([
            jnp.dot(normed, w_q, preferred_element_type=jnp.float32).astype(jnp.bfloat16),
            jnp.dot(normed, w_k, preferred_element_type=jnp.float32).astype(jnp.bfloat16),
            jnp.dot(normed, w_v, preferred_element_type=jnp.float32).astype(jnp.bfloat16),
        ], axis=1)
        projected = lax.psum_scatter(partials, "mx", scatter_dimension=0, tiled=True).astype(jnp.float32)
        row_count = projected.shape[0]
        kv_heads = kv_cols // HEAD
        q_vals = projected[:, :q_cols] + b_q.astype(jnp.float32)
        k_vals = projected[:, q_cols:q_cols + kv_cols] + b_k.astype(jnp.float32)
        v_vals = projected[:, q_cols + kv_cols:] + b_v.astype(jnp.float32)
        q_rot = apply_rotary(q_vals.reshape(row_count, q_cols // HEAD, HEAD), seq_lens).astype(jnp.bfloat16)
        k_rot = apply_rotary(k_vals.reshape(row_count, kv_heads, HEAD), seq_lens).astype(jnp.bfloat16)
        v_new = v_vals.reshape(row_count, kv_heads, HEAD).astype(jnp.bfloat16)
        at_slot = (jnp.arange(k_cache.shape[1])[None, :] == seq_lens[:, None])[:, :, None, None]
        k_cache_out = jnp.where(at_slot, k_rot[:, None], k_cache)
        v_cache_out = jnp.where(at_slot, v_new[:, None], v_cache)
        attn_rows = attend_local(q_rot, k_cache_out, v_cache_out, seq_lens)
        attn_all = lax.all_gather(attn_rows, "mx", axis=0, tiled=True)
        attn_proj = lax.psum(jnp.dot(attn_all, w_o, preferred_element_type=jnp.float32).astype(jnp.bfloat16), "my")
        x_mid = (x_f32 + attn_proj.astype(jnp.float32)).astype(jnp.bfloat16)
        mid_f32 = x_mid.astype(jnp.float32)
        mlp_sq = lax.psum(jnp.sum(mid_f32 * mid_f32, axis=1, keepdims=True), "mx")
        normed_mlp = (mid_f32 * lax.rsqrt(mlp_sq / hidden + NORM_EPS) * gain_mlp.astype(jnp.float32)).astype(jnp.bfloat16)
        ff_cols = w_gate.shape[1]
        gate_up = lax.psum(jnp.concatenate([
            jnp.dot(normed_mlp, w_gate, preferred_element_type=jnp.float32).astype(jnp.bfloat16),
            jnp.dot(normed_mlp, w_up, preferred_element_type=jnp.float32).astype(jnp.bfloat16),
        ], axis=1), "mx").astype(jnp.float32)
        hidden_act = (jax.nn.silu(gate_up[:, :ff_cols]) * gate_up[:, ff_cols:]).astype(jnp.bfloat16)
        down_proj = lax.psum(jnp.dot(hidden_act, w_down, preferred_element_type=jnp.float32).astype(jnp.bfloat16), "my")
        x_out = (mid_f32 + down_proj.astype(jnp.float32)).astype(jnp.bfloat16)
        return x_out, k_cache_out, v_cache_out

    return jax.shard_map(local_layer, mesh=mesh, in_specs=in_specs, out_specs=out_specs, check_vma=False)
```

profile of v0, /device:TPU:0, one launch (start us, length us, event | category | flops | bytes accessed | tf_op | source)
XLA Modules:
  0.0 321.3 jit_solution(12888799748982712284)
XLA Ops:
  7.2 0.0 copy-start
  7.2 0.0 reduce-scatter.2.cloned.1.call-start
  7.2 1.8 fusion.7
  9.0 3.0 psum.35
  12.0 0.8 convert_element_type.97
  12.8 2.0 convolution_convert_fusion.6
  14.9 0.6 convolution_convert_fusion.5
  15.5 0.7 copy-done.7
  16.2 1.9 convolution_convert_fusion.4
  18.2 1.0 pad_maximum_fusion.1
  19.2 0.0 reduce-scatter.2.cloned.1.call-update
  19.2 0.2 all-reduce.4.cloned.1.call-start
  19.5 0.2 multiply_cosine_fusion
  19.7 0.1 copy.28
  19.8 0.1 copy.29
  19.9 0.1 iota_compare_fusion.1
  20.0 7.1 %reduce-scatter.2.cloned.1.call-done = bf16[128,1792]{1,0:T(8,128)(2,1)} async-done(((bf16[256,1792]{1,0:T(8,128)(2,1)}), bf16[128,1792]{1,0:T(8,128)(2,1)}) %reduce-scatter.2.cloned.1.call-update) | async-done | bytes 458768 | tf_op jit(solution)/shard_map/reduce_scatter | solution.py:54
  27.1 1.1 convert_element_type.102
  28.3 0.2 copy.25
  28.5 0.1 subtract_convert_fusion
  28.6 0.1 reshape.145
  28.7 0.4 copy.27
  29.2 0.4 copy.26
  29.6 0.3 subtract_convert_fusion.1
  29.9 0.2 pad_maximum_fusion.2
  30.1 46.2 %broadcast_select_fusion.1 = (bf16[128,256,2,128]{3,2,1,0:T(2,128)(2,1)}, bf16[128,256,2,128]{3,2,1,0:T(2,128)(2,1)}) fusion(bf16[128,256,2,128]{3,2,1,0:T(2,128)(2,1)} %param.30, pred[128,256]{1,0:T(8,128)(4,1)S(1)} %get-tuple-element.16, bf16[128,2,128]{2,1,0:T(2,128)(2,1)S(1)} %pad_maximum_fusion.2, bf16[128,256,2,128]{3,2,1,0:T(2,128)(2,1)} %param.31, ...), kind=kLoop, calls=%fused_computation.1 | loop fusion | flops 16777216 | bytes 67272704 | tf_op jit(solution)/shard_map/jit(_where)/select_n | solution.py:64
  76.3 10.8 %fusion.15 = (f32[128,2,5]{2,1,0:T(2,128)S(1)}, f32[128,2,5,256]{3,2,1,0:T(8,128)S(1)}) fusion(pred[128,256]{1,0:T(8,128)(4,1)S(1)} %get-tuple-element.15, bf16[128,256,2,128]{3,2,1,0:T(2,128)(2,1)} %get-tuple-element.11, bf16[128,2,5,64]{3,2,1,0:T(8,128)(2,1)S(1)} %copy.27, bf16[128,2,5,64]{3,2,1,0:T(8,128)(2,1)S(1)} %copy.26), kind=kOutput, calls=%fused_computation.31 | convolution fusion | flops 85523200 | bytes 18453504 | tf_op jit(solution)/shard_map/bkgd,bskd->bkgs/dot_general | solution.py:26
  87.2 1.2 fusion.16
  88.4 8.1 %divide_convert_fusion = bf16[128,2,5,128]{3,2,1,0:T(8,128)(2,1)S(1)} fusion(bf16[128,256,2,128]{3,2,1,0:T(2,128)(2,1)} %get-tuple-element.12, f32[128,2,5,256]{3,2,1,0:T(8,128)S(1)} %get-tuple-element.18, f32[128,2,5]{2,1,0:T(2,128)S(1)} %get-tuple-element.17, pred[128,256]{1,0:T(8,128)(4,1)S(1)} %get-tuple-element.15, f32[128,2,5]{2,1,0:T(2,128)S(1)} %fusion.16), kind=kOutput, calls=%fused_computation.36 | convolution fusion | flops 85524480 | bytes 18458624 | tf_op jit(solution)/shard_map/bkgs,bskd->bkgd/dot_general | solution.py:31
  96.4 0.4 copy.32
  96.8 2.5 all_gather.3
  99.3 5.9 %convolution_convert_fusion.3 = bf16[256,2560]{1,0:T(8,128)(2,1)} fusion(bf16[256,1280]{0,1:T(8,128)(2,1)S(1)} %all_gather.3, bf16[1280,2560]{1,0:T(8,128)(2,1)} %param.26), kind=kOutput, calls=%fused_computation.18 | convolution fusion | flops 1678376960 | bytes 8519680 | tf_op jit(solution)/shard_map/dot_general | solution.py:68
  105.2 0.0 all-reduce.4.cloned.1.call-update
  105.3 0.0 all-reduce.6.cloned.1.call-start
  105.3 46.0 %all-reduce.4.cloned.1.call-done = bf16[256,2560]{1,0:T(8,128)(2,1)} async-done(((bf16[256,2560]{1,0:T(8,128)(2,1)}), bf16[256,2560]{1,0:T(8,128)(2,1)}) %all-reduce.4.cloned.1.call-update) | async-done | bytes 1310736 | tf_op jit(solution)/shard_map/psum | solution.py:68
  151.4 1.9 fusion.11
  153.3 2.5 psum.37
  155.7 16.6 %convolution_convert_fusion = bf16[256,6848]{0,1:T(8,128)(2,1)S(1)} fusion(bf16[2560,6848]{0,1:T(8,128)(2,1)} %param.28, bf16[256,2560]{1,0:T(8,128)(2,1)S(1)} %get-tuple-element.4, f32[2560]{0:T(1024)S(1)} %convert_element_type.115, f32[256]{0:T(256)S(1)} %bitcast.25), kind=kOutput, calls=%fused_computation.6 | convolution fusion | flops 8980185088 | bytes 39889920 | tf_op jit(solution)/shard_map/dot_general | solution.py:76
  172.3 16.6 %convolution_convert_fusion.1 = bf16[256,6848]{0,1:T(8,128)(2,1)S(1)} fusion(bf16[2560,6848]{0,1:T(8,128)(2,1)} %param.27, bf16[256,2560]{1,0:T(8,128)(2,1)S(1)} %get-tuple-element.4, f32[2560]{0:T(1024)S(1)} %convert_element_type.115, f32[256]{0:T(256)S(1)} %bitcast.26), kind=kOutput, calls=%fused_computation.7 | convolution fusion | flops 8980185088 | bytes 39889920 | tf_op jit(solution)/shard_map/dot_general | solution.py:75
  189.0 22.7 %pad_maximum_fusion = bf16[256,13696]{0,1:T(8,128)(2,1)} fusion(bf16[256,6848]{0,1:T(8,128)(2,1)S(1)} %convolution_convert_fusion, bf16[256,6848]{0,1:T(8,128)(2,1)S(1)} %convolution_convert_fusion.1), kind=kLoop, calls=%fused_computation.10 | loop fusion | flops 14024704 | bytes 14024704 | tf_op jit(solution)/shard_map/concatenate | solution.py:74
  211.7 0.0 all-reduce.6.cloned.1.call-update
  211.7 0.0 all-reduce.8.cloned.1.call-start
  211.8 25.3 %all-reduce.6.cloned.1.call-done = bf16[256,13696]{0,1:T(8,128)(2,1)} async-done(((bf16[256,13696]{0,1:T(8,128)(2,1)}), bf16[256,13696]{0,1:T(8,128)(2,1)}) %all-reduce.6.cloned.1.call-update) | async-done | bytes 7012368 | tf_op jit(solution)/shard_map/psum | solution.py:74
  237.1 8.1 %convert_element_type.119 = f32[256,13696]{0,1:T(8,128)} convert(bf16[256,13696]{0,1:T(8,128)(2,1)} %all-reduce.6.cloned.1.call-done) | non-fusion elementwise | flops 3506176 | bytes 21037056 | tf_op jit(solution)/shard_map/convert_element_type | solution.py:77
  245.3 20.7 %convolution_convert_fusion.2 = bf16[256,2560]{1,0:T(8,128)(2,1)} fusion(bf16[6848,2560]{1,0:T(8,128)(2,1)} %param.29, f32[256,13696]{0,1:T(8,128)} %convert_element_type.119), kind=kOutput, calls=%fused_computation.17 | convolution fusion | flops 8986984448 | bytes 50397184 | tf_op jit(solution)/shard_map/dot_general | solution.py:79
  265.9 0.0 all-reduce.8.cloned.1.call-update
  265.9 46.2 %all-reduce.8.cloned.1.call-done = bf16[256,2560]{1,0:T(8,128)(2,1)} async-done(((bf16[256,2560]{1,0:T(8,128)(2,1)}), bf16[256,2560]{1,0:T(8,128)(2,1)}) %all-reduce.8.cloned.1.call-update) | async-done | bytes 1310736 | tf_op jit(solution)/shard_map/psum | solution.py:79
  312.1 2.7 fusion.14
  (31 shorter events, 0.2 us)
Async XLA Ops:
  7.2 5.7 %copy-start = (bf16[2560,256]{1,0:T(8,128)(2,1)S(1)}, bf16[2560,256]{1,0:T(8,128)(2,1)}, u32[]{:S(2)}) copy-start(bf16[2560,256]{1,0:T(8,128)(2,1)} %param.22) | copy-start | bytes 3932164
  7.2 7.7 %copy-start.2 = (bf16[256,2560]{1,0:T(8,128)(2,1)S(1)}, bf16[256,2560]{1,0:T(8,128)(2,1)}, u32[]{:S(2)}) copy-start(bf16[256,2560]{1,0:T(8,128)(2,1)} %param.16) | copy-start | bytes 3932164
  7.2 19.9 %reduce-scatter.2.cloned.1.call-start = ((), (), s32[]{:S(2)}) async-start(), calls=%async_computation.1 | async-start | bytes 1376256 | tf_op jit(solution)/shard_map/reduce_scatter | solution.py:54
  12.0 2.9 copy-start.8
  12.8 3.4 %copy-start.7 = (bf16[2560,1280]{1,0:T(8,128)(2,1)S(1)}, bf16[2560,1280]{1,0:T(8,128)(2,1)}, u32[]{:S(2)}) copy-start(bf16[2560,1280]{1,0:T(8,128)(2,1)} %param.20) | copy-start | bytes 19660804
  18.1 1.3 copy-start.6
  18.1 1.3 copy-start.9
  18.2 1.3 copy-start.10
  18.2 1.3 copy-start.5
  19.2 132.2 %all-reduce.4.cloned.1.call-start = ((), (), s32[]{:S(2)}) async-start(), calls=%async_computation.2 | async-start | bytes 2621440 | tf_op jit(solution)/shard_map/psum | solution.py:68
  99.3 6.0 %copy-start.4 = (bf16[2560]{0:T(1024)(128)(2,1)S(1)}, bf16[2560]{0:T(1024)(128)(2,1)}, u32[]{:S(2)}) copy-start(bf16[2560]{0:T(1024)(128)(2,1)} %param.19) | copy-start | bytes 15364
  99.3 52.1 %copy-start.3 = (bf16[256,2560]{1,0:T(8,128)(2,1)S(1)}, bf16[256,2560]{1,0:T(8,128)(2,1)}, u32[]{:S(2)}) copy-start(bf16[256,2560]{1,0:T(8,128)(2,1)} %param.16) | copy-start | bytes 3932164
  105.3 131.8 %all-reduce.6.cloned.1.call-start = ((), (), s32[]{:S(2)}) async-start(), calls=%async_computation.3 | async-start | bytes 14024704 | tf_op jit(solution)/shard_map/psum | solution.py:74
  211.7 100.4 %all-reduce.8.cloned.1.call-start = ((), (), s32[]{:S(2)}) async-start(), calls=%async_computation.4 | async-start | bytes 2621440 | tf_op jit(solution)/shard_map/psum | solution.py:79
  265.9 48.9 %copy-start.1 = (bf16[2560,256]{1,0:T(8,128)(2,1)S(1)}, bf16[2560,256]{1,0:T(8,128)(2,1)}, u32[]{:S(2)}) copy-start(bf16[2560,256]{1,0:T(8,128)(2,1)} %param.22) | copy-start | bytes 3932164
Sparse Core Ops, SparseCore 0:
  19.3 7.7 reduce-scatter.1
  105.4 45.9 all-reduce.3
  211.9 25.2 all-reduce.5
  266.1 45.9 all-reduce.7
where the time goes:
time: 322 us; the launch traced here: 321 us
  waiting for transfers between devices  125 us (39%)
  other arithmetic  88.5 us (27%)
  matrix products  83.2 us (26%)
  between operations  14.1 us (4%)
  blocking collectives  7.95 us (2%)
    select_n x1, other arithmetic, local_layer(): k_cache_out = jnp.where(at_slot, k_rot[:, None], k_cache)  46.2 us
    psum x1, waiting for transfers between devices, local_layer(): lax.psum(jnp.dot(hidden_act, w_down, preferred_element_type=jnp.float32)....  46.2 us
    psum x1, waiting for transfers between devices, local_layer(): lax.psum(jnp.dot(attn_all, w_o, preferred_element_type=jnp.float32).astyp...  46 us
    psum x1, waiting for transfers between devices, local_layer(): lax.psum(jnp.concatenate([jnp.dot(normed_mlp, w_gate, preferred_element_t...  25.3 us
    concatenate x1, other arithmetic, local_layer(): jnp.concatenate([jnp.dot(normed_mlp, w_gate, preferred_element_type=jnp.f...  22.7 us
    dot_general x1, matrix products, local_layer(): jnp.dot(hidden_act, w_down, preferred_element_type=jnp.float32)  20.7 us
    dot_general x1, matrix products, local_layer(): jnp.dot(normed_mlp, w_gate, preferred_element_type=jnp.float32)  16.6 us
    dot_general x1, matrix products, local_layer(): jnp.dot(normed_mlp, w_up, preferred_element_type=jnp.float32)  16.6 us
  transfers between devices with their start and end apart: 4, of which 4 were waited for; matrix products, arithmetic and copies ran while one was open for 0% of the time, Pallas kernels for 0%

commit v1 on v0

v1 whole, which is shorter than its diff:
```python
import jax
import jax.numpy as jnp
from jax import lax
from jax.experimental import pallas as pl
from jax.experimental.pallas import tpu as pltpu
from jax.sharding import PartitionSpec as P

HEAD = 128
NORM_EPS = 1e-6
ROPE_THETA = 1000000.0
MESH = pl.DeviceIdType.MESH
F32 = jnp.float32
BF16 = jnp.bfloat16
QPAD = 16
VMEM = pltpu.VMEM
DMA = pltpu.SemaphoreType.DMA


def any_specs(count):
    return [pl.BlockSpec(memory_space=pl.ANY)] * count


def vmem_specs(count):
    return [pl.BlockSpec(memory_space=pltpu.VMEM)] * count


def project_kernel(x_ref, gain_ref, bias_ref, cos_ref, sin_ref, wq_hbm, wk_hbm, wv_hbm, q_out, kv_out,
                   w_buf, normed, sq_send, sq_recv, part_send, part_recv, part_own, w_sems, send_sems, recv_sems):
    me = lax.axis_index("mx")
    peer = 1 - me
    rows, depth = x_ref.shape
    half = rows // 2
    width = 2 * HEAD
    q_chunks = wq_hbm.shape[1] // width
    chunks = q_chunks + 2

    def weight_copy(index):
        if index < q_chunks:
            source = wq_hbm.at[:, pl.ds(index * width, width)]
        else:
            source = (wk_hbm, wv_hbm)[index - q_chunks]
        return pltpu.make_async_copy(source, w_buf.at[index], w_sems.at[index])

    for index in range(chunks):
        weight_copy(index).start()
    barrier = pltpu.get_barrier_semaphore()
    pl.semaphore_signal(barrier, inc=1, device_id={"mx": peer}, device_id_type=MESH)

    total = jnp.zeros((rows, HEAD), F32)
    for start in range(0, depth, HEAD):
        block = x_ref[:, start:start + HEAD].astype(F32)
        total = total + block * block
    sq_own = jnp.sum(total, axis=1, keepdims=True)
    sq_send[...] = jnp.broadcast_to(sq_own, (rows, HEAD))
    pl.semaphore_wait(barrier, 1)

    def remote(source, target, slot):
        return pltpu.make_async_remote_copy(
            src_ref=source, dst_ref=target, send_sem=send_sems.at[slot], recv_sem=recv_sems.at[slot],
            device_id={"mx": peer}, device_id_type=MESH)

    sq_copy = remote(sq_send, sq_recv, chunks)
    sq_copy.start()
    sq_copy.wait()
    scale = lax.rsqrt((sq_send[...] + sq_recv[...]) / (2 * depth) + NORM_EPS)
    for start in range(0, depth, HEAD):
        block = x_ref[:, start:start + HEAD].astype(F32)
        gain = gain_ref[:, start:start + HEAD].astype(F32)
        normed[:, start:start + HEAD] = (block * scale * gain).astype(BF16)

    own_rows = pl.ds(pl.multiple_of(me * half, half), half)
    peer_rows = pl.ds(pl.multiple_of(peer * half, half), half)
    copies = []
    for index in range(chunks):
        weight_copy(index).wait()
        weights = w_buf.at[index]
        part_send[index] = jnp.dot(normed[peer_rows, :], weights[...], preferred_element_type=F32).astype(BF16)
        part_own[index] = jnp.dot(normed[own_rows, :], weights[...], preferred_element_type=F32)
        copies.append(remote(part_send.at[index], part_recv.at[index], index))
        copies[index].start()

    cos_tab = cos_ref[...]
    sin_tab = sin_ref[...]
    for index in range(chunks):
        copies[index].wait()
        for head in range(2):
            lanes = slice(head * HEAD, (head + 1) * HEAD)
            columns = slice(index * width + head * HEAD, index * width + (head + 1) * HEAD)
            value = part_own[index][:, lanes] + part_recv[index][:, lanes].astype(F32) + bias_ref[:, columns].astype(F32)
            if index < chunks - 1:
                value = value * cos_tab + pltpu.roll(value, HEAD // 2, 1) * sin_tab
            if index < q_chunks:
                q_out[:, columns] = value.astype(BF16)
            else:
                kv_out[:, (index - q_chunks) * width + head * HEAD:(index - q_chunks) * width + (head + 1) * HEAD] = value.astype(BF16)


def project(x_in, gain, bias, cos_tab, sin_tab, w_q, w_k, w_v):
    rows, depth = x_in.shape
    half = rows // 2
    width = 2 * HEAD
    chunks = w_q.shape[1] // width + 2
    return pl.pallas_call(
        project_kernel,
        name="project",
        out_shape=(jax.ShapeDtypeStruct((half, w_q.shape[1]), BF16), jax.ShapeDtypeStruct((half, 2 * width), BF16)),
        in_specs=vmem_specs(5) + any_specs(3),
        out_specs=tuple(vmem_specs(2)),
        scratch_shapes=[
            VMEM((chunks, depth, width), BF16),
            VMEM((rows, depth), BF16),
            VMEM((rows, HEAD), F32),
            VMEM((rows, HEAD), F32),
            VMEM((chunks, half, width), BF16),
            VMEM((chunks, half, width), BF16),
            VMEM((chunks, half, width), F32),
            DMA((chunks,)),
            DMA((chunks + 1,)),
            DMA((chunks + 1,)),
        ],
        compiler_params=pltpu.CompilerParams(collective_id=0, has_side_effects=True, vmem_limit_bytes=48 << 20),
    )(x_in, gain, bias, cos_tab, sin_tab, w_q, w_k, w_v)


SLOTS = 4
ROWS_STEP = 8


def attend_kernel(lens_ref, q_ref, kv_ref, k_hbm, v_hbm, o_ref, k_out, v_out,
                  k_buf, v_buf, q_wide, q_packed, kv_wide, o_wide, parity, scores, weights, sums, in_sems, out_sems):
    batch, kv_rows, _ = k_hbm.shape
    q_heads = q_ref.shape[1] // HEAD
    group = q_heads // 2
    steps = batch // ROWS_STEP

    def load(step, kind):
        slot = lax.rem(step, SLOTS)
        source, target = ((k_hbm, k_buf), (v_hbm, v_buf))[kind]
        return pltpu.make_async_copy(source.at[pl.ds(step * ROWS_STEP, ROWS_STEP)], target.at[slot], in_sems.at[kind, slot])

    def save(step, kind):
        slot = lax.rem(step, SLOTS)
        source, target = ((k_buf, k_out), (v_buf, v_out))[kind]
        return pltpu.make_async_copy(source.at[slot], target.at[pl.ds(step * ROWS_STEP, ROWS_STEP)], out_sems.at[kind, slot])

    for step in range(2):
        for kind in range(2):
            load(step, kind).start()

    q_wide[...] = jnp.zeros_like(q_wide)
    for head in range(q_heads):
        q_wide[pl.ds(head, batch, stride=QPAD), :] = q_ref[:, head * HEAD:(head + 1) * HEAD].astype(F32)
    q_packed[...] = q_wide[...].astype(BF16)
    for kind in range(2):
        for head in range(2):
            start = (kind * 2 + head) * HEAD
            kv_wide[kind, pl.ds(head, batch, stride=2), :] = kv_ref[:, start:start + HEAD].astype(F32)
    row_head = lax.broadcasted_iota(jnp.int32, (QPAD, kv_rows), 0) >= group
    col_head = lax.rem(lax.broadcasted_iota(jnp.int32, (QPAD, kv_rows), 1), 2) == 1
    parity[...] = jnp.where(row_head == col_head, 0.0, -jnp.inf)
    columns = lax.broadcasted_iota(jnp.int32, (QPAD, kv_rows), 1)
    tile_row = lax.broadcasted_iota(jnp.int32, (16, HEAD), 0)
    tile_pos = lax.div(tile_row, 2)
    tile_odd = lax.rem(tile_row, 2) == 1

    def body(step, carry):
        slot = lax.rem(step, SLOTS)

        @pl.when(step + 2 < steps)
        def _():
            @pl.when(step >= 2)
            def _():
                for kind in range(2):
                    save(step - 2, kind).wait()
            for kind in range(2):
                load(step + 2, kind).start()

        for kind in range(2):
            load(step, kind).wait()
        for row in range(ROWS_STEP):
            index = step * ROWS_STEP + row
            position = lens_ref[index]
            base = pl.multiple_of(lax.div(position, 8) * 16, 16)
            offset = lax.rem(position, 8)
            for kind, buffer in ((0, k_buf), (1, v_buf)):
                low = kv_wide[kind, pl.ds(2 * index, 1), :]
                high = kv_wide[kind, pl.ds(2 * index + 1, 1), :]
                fresh = jnp.where(tile_odd, high, low).astype(BF16)
                tile = buffer[slot, row, pl.ds(base, 16), :]
                buffer[slot, row, pl.ds(base, 16), :] = jnp.where(tile_pos == offset, fresh, tile)
        for row in range(ROWS_STEP):
            q_start = pl.multiple_of((step * ROWS_STEP + row) * QPAD, QPAD)
            scores[row] = lax.dot_general(q_packed[pl.ds(q_start, QPAD), :], k_buf[slot, row], (((1,), (1,)), ((), ())),
                                          preferred_element_type=F32)
        for kind in range(2):
            save(step, kind).start()
        for row in range(ROWS_STEP):
            limit = 2 * lens_ref[step * ROWS_STEP + row] + 2
            masked = jnp.where(columns < limit, scores[row] * HEAD ** -0.5 + parity[...], -jnp.inf)
            weight = jnp.exp(masked - jnp.max(masked, axis=1, keepdims=True))
            sums[row] = jnp.broadcast_to(jnp.sum(weight, axis=1, keepdims=True), (QPAD, HEAD))
            weights[row] = weight.astype(BF16)
        for row in range(ROWS_STEP):
            q_start = pl.multiple_of((step * ROWS_STEP + row) * QPAD, QPAD)
            mixed = jnp.dot(weights[row], v_buf[slot, row], preferred_element_type=F32)
            o_wide[pl.ds(q_start, QPAD), :] = mixed / sums[row]
        return carry

    lax.fori_loop(0, steps, body, 0)
    for head in range(q_heads):
        o_ref[:, head * HEAD:(head + 1) * HEAD] = o_wide[pl.ds(head, batch, stride=QPAD), :].astype(BF16)
    for step in range(steps - SLOTS, steps):
        for kind in range(2):
            save(step, kind).wait()


def attend(seq_lens, q_rot, kv_new, k_cache, v_cache):
    batch, seq_len, kv_heads, _ = k_cache.shape
    rows = seq_len * kv_heads
    flat = (batch, rows, HEAD)
    out, k_out, v_out = pl.pallas_call(
        attend_kernel,
        name="attend",
        out_shape=(jax.ShapeDtypeStruct(q_rot.shape, BF16), jax.ShapeDtypeStruct(flat, BF16), jax.ShapeDtypeStruct(flat, BF16)),
        in_specs=[pl.BlockSpec(memory_space=pltpu.SMEM)] + vmem_specs(2) + any_specs(2),
        out_specs=tuple(vmem_specs(1) + any_specs(2)),
        scratch_shapes=[
            VMEM((SLOTS, ROWS_STEP, rows, HEAD), BF16),
            VMEM((SLOTS, ROWS_STEP, rows, HEAD), BF16),
            VMEM((batch * QPAD, HEAD), F32),
            VMEM((batch * QPAD, HEAD), BF16),
            VMEM((2, batch * 2, HEAD), F32),
            VMEM((batch * QPAD, HEAD), F32),
            VMEM((QPAD, rows), F32),
            VMEM((ROWS_STEP, QPAD, rows), F32),
            VMEM((ROWS_STEP, QPAD, rows), BF16),
            VMEM((ROWS_STEP, QPAD, HEAD), F32),
            DMA((2, SLOTS)),
            DMA((2, SLOTS)),
        ],
        compiler_params=pltpu.CompilerParams(vmem_limit_bytes=48 << 20),
    )(seq_lens, q_rot, kv_new, k_cache.reshape(flat), v_cache.reshape(flat))
    return out, k_out.reshape(k_cache.shape), v_out.reshape(v_cache.shape)


def rotary_tables(positions):
    half_dim = HEAD // 2
    inv_freq = ROPE_THETA ** (-2.0 * jnp.arange(half_dim, dtype=F32) / HEAD)
    angles = positions.astype(F32)[:, None] * jnp.concatenate([inv_freq, inv_freq])
    sign = jnp.where(jnp.arange(HEAD) < half_dim, -1.0, 1.0)
    return jnp.cos(angles), jnp.sin(angles) * sign


def solution(mesh):
    mx_size = mesh.shape["mx"]
    act_spec = P(None, "mx")
    cache_spec = P("mx", None, "my", None)
    in_specs = (act_spec, P("mx"), P("mx"), P("mx"), P("mx", "my"), P("my"), P("mx", "my"), P("my"), P("mx", "my"), P("my"), P("my", "mx"), P("mx", "my"), P("mx", "my"), P("my", "mx"), cache_spec, cache_spec)
    out_specs = (act_spec, cache_spec, cache_spec)

    def local_layer(x_in, seq_lens, gain_attn, gain_mlp, w_q, b_q, w_k, b_k, w_v, b_v, w_o, w_gate, w_up, w_down, k_cache, v_cache):
        hidden = x_in.shape[1] * mx_size
        x_f32 = x_in.astype(F32)
        cos_tab, sin_tab = rotary_tables(seq_lens)
        bias = jnp.concatenate([b_q, b_k, b_v])[None, :]
        q_rot, kv_new = project(x_in, gain_attn[None, :], bias, cos_tab, sin_tab, w_q, w_k, w_v)
        attn_rows, k_cache_out, v_cache_out = attend(seq_lens, q_rot, kv_new, k_cache, v_cache)
        attn_all = lax.all_gather(attn_rows, "mx", axis=0, tiled=True)
        attn_proj = lax.psum(jnp.dot(attn_all, w_o, preferred_element_type=F32).astype(BF16), "my")
        x_mid = (x_f32 + attn_proj.astype(F32)).astype(BF16)
        mid_f32 = x_mid.astype(F32)
        mlp_sq = lax.psum(jnp.sum(mid_f32 * mid_f32, axis=1, keepdims=True), "mx")
        normed_mlp = (mid_f32 * lax.rsqrt(mlp_sq / hidden + NORM_EPS) * gain_mlp.astype(F32)).astype(BF16)
        ff_cols = w_gate.shape[1]
        gate_up = lax.psum(jnp.concatenate([
            jnp.dot(normed_mlp, w_gate, preferred_element_type=F32).astype(BF16),
            jnp.dot(normed_mlp, w_up, preferred_element_type=F32).astype(BF16),
        ], axis=1), "mx").astype(F32)
        hidden_act = (jax.nn.silu(gate_up[:, :ff_cols]) * gate_up[:, ff_cols:]).astype(BF16)
        down_proj = lax.psum(jnp.dot(hidden_act, w_down, preferred_element_type=F32).astype(BF16), "my")
        x_out = (mid_f32 + down_proj.astype(F32)).astype(BF16)
        return x_out, k_cache_out, v_cache_out

    return jax.shard_map(local_layer, mesh=mesh, in_specs=in_specs, out_specs=out_specs, check_vma=False)
```

time: 322 us -> 269 us (0.84)
  other arithmetic: 88.5 us -> 37.1 us
  Pallas kernels: 0 us -> 32.1 us
  matrix products: 83.2 us -> 56.8 us
  waiting for transfers between devices: 125 us -> 119 us
    select_n x1, other arithmetic: 46.2 us -> 0.07 us  [rotary_tables(): sign = jnp.where(jnp.arange(HEAD) < half_dim, -1.0, 1.0)]
    pallas_call x0 -> x2, Pallas kernels: none -> 32.1 us  [the longest x1 24.8 us: attend(): pl.pallas_call(attend_kernel, name='attend', out_shape=(jax.ShapeDtypeStr...]
    dot_general x9 -> x4, matrix products: 83.2 us -> 56.8 us  [the longest x1 20.7 us: local_layer(): jnp.dot(hidden_act, w_down, preferred_element_type=F32).astype(BF16)]
    reduce_scatter x1 -> x0, waiting for transfers between devices: 7.1 us -> none  [local_layer(): lax.psum_scatter(partials, 'mx', scatter_dimension=0, tiled=True)]
    concatenate x3 -> x2, other arithmetic: 23.9 us -> 23.4 us  [the longest x1 22.7 us: local_layer(): jnp.concatenate([jnp.dot(normed_mlp, w_gate, preferred_element_type=F32)....]
  transfers between devices with their start and end apart: 4 -> 3, of which waited for: 4 -> 3; matrix products, arithmetic and copies ran while one was open for 0% -> 0% of each run, Pallas kernels for 0% -> 0%
where the time goes in v1:
time: 269 us; the launch traced here: 268 us
  waiting for transfers between devices  119 us (44%)
  matrix products  56.8 us (21%)
  other arithmetic  37.1 us (14%)
  Pallas kernels  32.1 us (12%)
  between operations  13.8 us (5%)
  blocking collectives  4.92 us (2%)
  local copies, waits for them, and re-layouts  4.68 us (2%)
    psum x1, waiting for transfers between devices, local_layer(): lax.psum(jnp.dot(attn_all, w_o, preferred_element_type=F32).astype(BF16),...  47.2 us
    psum x1, waiting for transfers between devices, local_layer(): lax.psum(jnp.dot(hidden_act, w_down, preferred_element_type=F32).astype(B...  46.2 us
    psum x1, waiting for transfers between devices, local_layer(): lax.psum(jnp.concatenate([jnp.dot(normed_mlp, w_gate, preferred_element_t...  25.3 us
    pallas_call x1, Pallas kernels, attend(): pl.pallas_call(attend_kernel, name='attend', out_shape=(jax.ShapeDtypeStr...  24.8 us
    concatenate x1, other arithmetic, local_layer(): jnp.concatenate([jnp.dot(normed_mlp, w_gate, preferred_element_type=F32)....  22.7 us
    dot_general x1, matrix products, local_layer(): jnp.dot(hidden_act, w_down, preferred_element_type=F32).astype(BF16)  20.7 us
    dot_general x1, matrix products, local_layer(): jnp.dot(normed_mlp, w_gate, preferred_element_type=F32).astype(BF16)  16.6 us
    dot_general x1, matrix products, local_layer(): jnp.dot(normed_mlp, w_up, preferred_element_type=F32).astype(BF16)  16.6 us
  transfers between devices with their start and end apart: 3, of which 3 were waited for; matrix products, arithmetic and copies ran while one was open for 0% of the time, Pallas kernels for 0%

profile of v1, /device:TPU:0, one launch (start us, length us, event | category | flops | bytes accessed | tf_op | source)
XLA Modules:
  0.0 268.4 jit_solution(9011077461492028054)
XLA Ops:
  7.2 0.0 all-reduce.4.cloned.1.call-start
  7.2 0.7 convert_element_type.46
  7.9 0.1 compare_select_fusion
  8.0 0.7 pad_maximum_fusion.1
  8.7 0.7 broadcast_in_dim.21.gain_ref
  9.4 0.3 fusion.9
  9.7 0.0 copy-start
  9.7 1.3 copy-done
  11.0 0.0 copy-start.2
  11.0 1.3 copy-done.2
  12.3 0.0 copy-start.3
  12.3 1.3 copy-done.3
  13.7 0.0 copy-start.4
  13.7 0.0 slice-start
  13.7 7.3 %project.1 = (bf16[128,1280]{1,0:T(8,128)(2,1)S(1)}, bf16[128,512]{1,0:T(8,128)(2,1)S(1)}) custom-call(bf16[256,2560]{1,0:T(8,128)(2,1)S(1)} %copy-done, bf16[1,2560]{1,0:T(2,128)(2,1)S(1)} %broadcast_in_dim.21.gain_ref, bf16[1,1792]{1,0:T(2,128)(2,1)S(1)} %broadcast_in_dim.22.bias_ref, f32[128,128]{1,0:T(8,128)S(1)} %get-tuple-element.16.cos_ref, ...), custom_call_target="tpu_custom_call" | custom-call | tf_op jit(solution)/shard_map/project/pallas_call | solution.py:103
  21.0 0.0 copy-done.4
  21.0 0.0 slice-start.1
  21.0 24.8 %attend.1 = (bf16[128,1280]{1,0:T(8,128)(2,1)S(1)}, bf16[128,512,128]{2,1,0:T(8,128)(2,1)}, bf16[128,512,128]{2,1,0:T(8,128)(2,1)}) custom-call(s32[128]{0:T(128)S(1)} %copy-done.4, bf16[128,1280]{1,0:T(8,128)(2,1)S(1)} %get-tuple-element.8.q_ref, bf16[128,512]{1,0:T(8,128)(2,1)S(1)} %get-tuple-element.9.kv_ref, bf16[128,512,128]{2,1,0:T(8,128)(2,1)} %bitcast.11, ...), custom_call_target="tpu_custom_call" | custom-call | tf_op jit(solution)/shard_map/attend/pallas_call | solution.py:221
  45.8 2.3 all_gather.3
  48.1 0.0 slice-done
  48.1 0.0 slice-done.1
  48.1 0.0 copy-start.5
  48.1 0.0 copy-start.1
  48.1 2.9 %convolution_convert_fusion.3 = bf16[256,2560]{1,0:T(8,128)(2,1)} fusion(bf16[256,1280]{1,0:T(8,128)(2,1)S(1)} %all_gather.3, bf16[1280,2560]{1,0:T(8,128)(2,1)S(1)} %bitcast.19), kind=kOutput, calls=%fused_computation.9 | convolution fusion | flops 1678376960 | bytes 8519680 | tf_op jit(solution)/shard_map/dot_general | solution.py:269
  51.0 0.0 all-reduce.4.cloned.1.call-update
  51.1 0.0 all-reduce.6.cloned.1.call-start
  51.1 0.0 copy-done.5
  51.1 47.2 %all-reduce.4.cloned.1.call-done = bf16[256,2560]{1,0:T(8,128)(2,1)} async-done(((bf16[256,2560]{1,0:T(8,128)(2,1)}), bf16[256,2560]{1,0:T(8,128)(2,1)}) %all-reduce.4.cloned.1.call-update) | async-done | bytes 1310736 | tf_op jit(solution)/shard_map/psum | solution.py:269
  98.4 0.0 copy-done.1
  98.4 1.9 fusion.3
  100.2 2.6 psum.29
  102.9 16.6 %convolution_convert_fusion = bf16[256,6848]{0,1:T(8,128)(2,1)S(1)} fusion(bf16[2560,6848]{0,1:T(8,128)(2,1)} %param.28, bf16[256,2560]{1,0:T(8,128)(2,1)S(1)} %get-tuple-element.14, f32[2560]{0:T(1024)S(1)} %convert_element_type.51, f32[256]{0:T(256)S(1)} %bitcast.14), kind=kOutput, calls=%fused_computation | convolution fusion | flops 8980185088 | bytes 39889920 | tf_op jit(solution)/shard_map/dot_general | solution.py:277
  119.5 16.6 %convolution_convert_fusion.1 = bf16[256,6848]{0,1:T(8,128)(2,1)S(1)} fusion(bf16[2560,6848]{0,1:T(8,128)(2,1)} %param.27, bf16[256,2560]{1,0:T(8,128)(2,1)S(1)} %get-tuple-element.14, f32[2560]{0:T(1024)S(1)} %convert_element_type.51, f32[256]{0:T(256)S(1)} %bitcast.15), kind=kOutput, calls=%fused_computation.1 | convolution fusion | flops 8980185088 | bytes 39889920 | tf_op jit(solution)/shard_map/dot_general | solution.py:276
  136.1 22.7 %pad_maximum_fusion = bf16[256,13696]{0,1:T(8,128)(2,1)} fusion(bf16[256,6848]{0,1:T(8,128)(2,1)S(1)} %convolution_convert_fusion, bf16[256,6848]{0,1:T(8,128)(2,1)S(1)} %convolution_convert_fusion.1), kind=kLoop, calls=%fused_computation.4 | loop fusion | flops 14024704 | bytes 14024704 | tf_op jit(solution)/shard_map/concatenate | solution.py:275
  158.8 0.0 all-reduce.6.cloned.1.call-update
  158.8 0.0 all-reduce.8.cloned.1.call-start
  158.9 25.3 %all-reduce.6.cloned.1.call-done = bf16[256,13696]{0,1:T(8,128)(2,1)} async-done(((bf16[256,13696]{0,1:T(8,128)(2,1)}), bf16[256,13696]{0,1:T(8,128)(2,1)}) %all-reduce.6.cloned.1.call-update) | async-done | bytes 7012368 | tf_op jit(solution)/shard_map/psum | solution.py:275
  184.2 8.1 %convert_element_type.55 = f32[256,13696]{0,1:T(8,128)} convert(bf16[256,13696]{0,1:T(8,128)(2,1)} %all-reduce.6.cloned.1.call-done) | non-fusion elementwise | flops 3506176 | bytes 21037056 | tf_op jit(solution)/shard_map/convert_element_type | solution.py:278
  192.3 20.7 %convolution_convert_fusion.2 = bf16[256,2560]{1,0:T(8,128)(2,1)} fusion(bf16[6848,2560]{1,0:T(8,128)(2,1)} %param.29, f32[256,13696]{0,1:T(8,128)} %convert_element_type.55), kind=kOutput, calls=%fused_computation.8 | convolution fusion | flops 8986984448 | bytes 50397184 | tf_op jit(solution)/shard_map/dot_general | solution.py:280
  213.0 0.0 all-reduce.8.cloned.1.call-update
  213.0 46.2 %all-reduce.8.cloned.1.call-done = bf16[256,2560]{1,0:T(8,128)(2,1)} async-done(((bf16[256,2560]{1,0:T(8,128)(2,1)}), bf16[256,2560]{1,0:T(8,128)(2,1)}) %all-reduce.8.cloned.1.call-update) | async-done | bytes 1310736 | tf_op jit(solution)/shard_map/psum | solution.py:280
  259.2 2.7 fusion.6
  (5 shorter events, 0.0 us)
Async XLA Ops:
  7.2 91.2 %all-reduce.4.cloned.1.call-start = ((), (), s32[]{:S(2)}) async-start(), calls=%async_computation | async-start | bytes 2621440 | tf_op jit(solution)/shard_map/psum | solution.py:269
  9.7 1.3 copy-start
  11.0 1.3 copy-start.2
  12.3 1.3 copy-start.3
  13.7 7.3 %copy-start.4 = (s32[128]{0:T(128)S(1)}, s32[128]{0:T(128)}, u32[]{:S(2)}) copy-start(s32[128]{0:T(128)} %lens_ref.1) | copy-start | bytes 1540
  13.7 34.4 %slice-start = ((s8[6553600]{0:T(1024)(128)(4,1)}), s8[2359296]{0:T(1024)(128)(4,1)S(1)}, s32[]{:S(2)}) async-start(s8[6553600]{0:T(1024)(128)(4,1)} %bitcast.18), calls=%async_computation.3 | async-start | bytes 4718592
  21.0 27.1 %slice-start.1 = ((s8[6553600]{0:T(1024)(128)(4,1)}), s8[4194304]{0:T(1024)(128)(4,1)S(1)}, s32[]{:S(2)}) async-start(s8[6553600]{0:T(1024)(128)(4,1)} %bitcast.18), calls=%async_computation.4 | async-start | bytes 8388608
  48.1 3.0 %copy-start.5 = (bf16[2560]{0:T(1024)(128)(2,1)S(1)}, bf16[2560]{0:T(1024)(128)(2,1)}, u32[]{:S(2)}) copy-start(bf16[2560]{0:T(1024)(128)(2,1)} %param.19) | copy-start | bytes 15364
  48.1 50.2 %copy-start.1 = (bf16[256,2560]{1,0:T(8,128)(2,1)S(1)}, bf16[256,2560]{1,0:T(8,128)(2,1)}, u32[]{:S(2)}) copy-start(bf16[256,2560]{1,0:T(8,128)(2,1)} %x_ref.1) | copy-start | bytes 3932164
  51.1 133.1 %all-reduce.6.cloned.1.call-start = ((), (), s32[]{:S(2)}) async-start(), calls=%async_computation.1 | async-start | bytes 14024704 | tf_op jit(solution)/shard_map/psum | solution.py:275
  158.8 100.3 %all-reduce.8.cloned.1.call-start = ((), (), s32[]{:S(2)}) async-start(), calls=%async_computation.2 | async-start | bytes 2621440 | tf_op jit(solution)/shard_map/psum | solution.py:280
Sparse Core Ops, SparseCore 0:
  51.2 47.1 all-reduce.3
  159.0 25.2 all-reduce.5
  213.1 45.9 all-reduce.7

commit v2 on v1

--- a/solution.py
+++ b/solution.py
@@ -118,7 +118,7 @@
             DMA((chunks + 1,)),
             DMA((chunks + 1,)),
         ],
-        compiler_params=pltpu.CompilerParams(collective_id=0, has_side_effects=True, vmem_limit_bytes=48 << 20),
+        compiler_params=pltpu.CompilerParams(collective_id=0, has_side_effects=True, vmem_limit_bytes=67043328),
     )(x_in, gain, bias, cos_tab, sin_tab, w_q, w_k, w_v)
 
 
@@ -238,9 +238,374 @@
             DMA((2, SLOTS)),
             DMA((2, SLOTS)),
         ],
-        compiler_params=pltpu.CompilerParams(vmem_limit_bytes=48 << 20),
+        compiler_params=pltpu.CompilerParams(vmem_limit_bytes=64 << 20),
     )(seq_lens, q_rot, kv_new, k_cache.reshape(flat), v_cache.reshape(flat))
     return out, k_out.reshape(k_cache.shape), v_out.reshape(v_cache.shape)
+
+
+BLOCK = 256
+RING = 36
+
+
+def tail_kernel(attn_ref, gain_ref, x_hbm, wo_hbm, wg_hbm, wu_hbm, wd_hbm, out_ref,
+                pool, full, rows_in, part, keep, recv_one, send_two, recv_two, x_own, mid, sq_send, sq_recv,
+                h_rows, h_cols, gu_send, gu_recv, gu_own, act, early,
+                pool_sems, x_sem, core_sems, rs_sems, ag_sems, gu_sems, act_sems):
+    my = lax.axis_index("my")
+    me = lax.axis_index("mx")
+    peer = 1 - me
+    side_x = my + 1 - 2 * lax.rem(my, 2)
+    side_y = lax.rem(my + 2, 4)
+    cross = 3 - my
+    half, depth = attn_ref.shape
+    batch = 2 * half
+    quarter = batch // 4
+    hidden = x_hbm.shape[1]
+    ff = wg_hbm.shape[0]
+    col_chunks = hidden // BLOCK
+    ff_chunks = pl.cdiv(ff, BLOCK)
+    ff_rest = ff - (ff_chunks - 1) * BLOCK
+    chunk_ring = RING // 2
+    out_blocks = depth // BLOCK
+    out_slot = RING - 6
+
+    def slot_rows(slot, count=BLOCK):
+        return pl.ds(pl.multiple_of(slot * BLOCK, BLOCK), count)
+
+    def block_copy(source, block, slot, count=BLOCK):
+        return pltpu.make_async_copy(source.at[slot_rows(block, count)], pool.at[slot_rows(slot, count)], pool_sems.at[slot])
+
+    def ff_copies(chunk, count=BLOCK):
+        slot = 2 * lax.rem(chunk, chunk_ring)
+        return block_copy(wg_hbm, chunk, slot, count), block_copy(wu_hbm, chunk, slot + 1, count)
+
+    def down_copy(block, count=BLOCK):
+        return block_copy(wd_hbm, block, lax.rem(2 * ff_chunks + block, RING), count)
+
+    def out_copy(block):
+        return block_copy(wo_hbm, block, out_slot + block)
+
+    def to_core(source, target, slot):
+        return pltpu.make_async_remote_copy(src_ref=source, dst_ref=target, send_sem=slot[0], recv_sem=slot[1],
+                                            device_id={"mx": peer}, device_id_type=MESH)
+
+    def to_chip(source, target, chip, send_sem, recv_sem):
+        return pltpu.make_async_remote_copy(src_ref=source, dst_ref=target, send_sem=send_sem, recv_sem=recv_sem,
+                                            device_id={"my": chip}, device_id_type=MESH)
+
+    for block in range(out_blocks):
+        out_copy(block).start()
+    own_rows = pl.ds(pl.multiple_of(my * quarter, quarter), quarter)
+    x_copy = pltpu.make_async_copy(x_hbm.at[own_rows], x_own, x_sem)
+    x_copy.start()
+    for chunk in range(out_slot // 2):
+        for copy in ff_copies(chunk):
+            copy.start()
+
+    barrier = pltpu.get_barrier_semaphore()
+    pl.semaphore_signal(barrier, inc=1, device_id={"mx": peer}, device_id_type=MESH)
+    pl.semaphore_signal(barrier, inc=1, device_id={"my": side_x}, device_id_type=MESH)
+    pl.semaphore_signal(barrier, inc=1, device_id={"my": side_y}, device_id_type=MESH)
+    pl.semaphore_wait(barrier, 3)
+
+    own_half = pl.ds(pl.multiple_of(me * half, half), half)
+    peer_half = pl.ds(pl.multiple_of(peer * half, half), half)
+    attn_copy = to_core(attn_ref, full.at[own_half], (core_sems.at[0], core_sems.at[1]))
+    attn_copy.start()
+    full[own_half, :] = attn_ref[...]
+    attn_copy.wait()
+    for place, owner in enumerate((my, side_x, cross, side_y)):
+        rows_in[place * quarter:(place + 1) * quarter, :] = full[pl.ds(pl.multiple_of(owner * quarter, quarter), quarter), :]
+
+    def columns(chunk):
+        return slice(chunk * BLOCK, (chunk + 1) * BLOCK)
+
+    def first_side(chunk):
+        return (side_x, side_y)[chunk % 2]
+
+    def second_side(chunk):
+        return (side_y, side_x)[chunk % 2]
+
+    def scatter_one(stage, chunk):
+        sems = rs_sems.at[stage, 0]
+        return to_chip(part.at[chunk], recv_one.at[chunk], first_side(chunk), sems.at[0, chunk], sems.at[1, chunk])
+
+    def scatter_two(stage, chunk):
+        sems = rs_sems.at[stage, 1]
+        return to_chip(send_two.at[chunk], recv_two.at[chunk], second_side(chunk), sems.at[0, chunk], sems.at[1, chunk])
+
+    def scatter_start(stage, chunk, total):
+        lead = quarter * (1 + chunk % 2)
+        part[chunk] = total[lead:lead + 2 * quarter].astype(BF16)
+        keep[chunk, 0] = total[:quarter]
+        other = 3 * quarter if chunk % 2 == 0 else quarter
+        keep[chunk, 1] = total[other:other + quarter]
+        scatter_one(stage, chunk).start()
+
+    def scatter_pass(stage, chunk):
+        scatter_one(stage, chunk).wait()
+        mine = slice(0, quarter) if chunk % 2 == 0 else slice(quarter, 2 * quarter)
+        theirs = slice(quarter, 2 * quarter) if chunk % 2 == 0 else slice(0, quarter)
+        send_two[chunk] = (keep[chunk, 1] + recv_one[chunk, theirs, :].astype(F32)).astype(BF16)
+        scatter_two(stage, chunk).start()
+        keep[chunk, 0] = keep[chunk, 0] + recv_one[chunk, mine, :].astype(F32)
+
+    def scatter_end(stage, chunk):
+        scatter_two(stage, chunk).wait()
+        return keep[chunk, 0] + recv_two[chunk].astype(F32)
+
+    def mid_end(chunk):
+        mid[:, columns(chunk)] = (x_own[:, columns(chunk)].astype(F32) + scatter_end(0, chunk)).astype(BF16).astype(F32)
+
+    x_copy.wait()
+    for block in range(out_blocks):
+        out_copy(block).wait()
+    for chunk in range(col_chunks):
+        weights = pool[out_slot * BLOCK:out_slot * BLOCK + depth, columns(chunk)]
+        scatter_start(0, chunk, jnp.dot(rows_in[...], weights, preferred_element_type=F32))
+        if chunk >= 3:
+            scatter_pass(0, chunk - 3)
+        if chunk >= 7:
+            mid_end(chunk - 7)
+    for chunk in range(out_slot // 2, chunk_ring):
+        for copy in ff_copies(chunk):
+            copy.start()
+    for chunk in range(col_chunks, col_chunks + 7):
+        if chunk - 3 < col_chunks:
+            scatter_pass(0, chunk - 3)
+        mid_end(chunk - 7)
+
+    square = jnp.zeros((quarter, HEAD), F32)
+    for start in range(0, hidden, HEAD):
+        square = square + mid[:, start:start + HEAD] * mid[:, start:start + HEAD]
+    sq_send[...] = jnp.broadcast_to(jnp.sum(square, axis=1, keepdims=True), (quarter, HEAD))
+    sq_copy = to_core(sq_send, sq_recv, (core_sems.at[2], core_sems.at[3]))
+    sq_copy.start()
+    sq_copy.wait()
+    scale = lax.rsqrt((sq_send[...] + sq_recv[...]) / (2 * hidden) + NORM_EPS)
+
+    def place_rows(place):
+        return slice(place * quarter, (place + 1) * quarter)
+
+    def gather_x(chunk):
+        return to_chip(h_rows.at[place_rows(0), columns(chunk)], h_rows.at[place_rows(1), columns(chunk)], side_x,
+                       ag_sems.at[0, 0, 0, chunk], ag_sems.at[0, 0, 1, chunk])
+
+    def gather_y(chunk):
+        return to_chip(h_rows.at[place_rows(0), columns(chunk)], h_rows.at[place_rows(3), columns(chunk)], side_y,
+                       ag_sems.at[0, 1, 0, chunk], ag_sems.at[0, 1, 1, chunk])
+
+    def gather_cross(chunk):
+        source = 1 if chunk % 2 == 0 else 3
+        return to_chip(h_rows.at[place_rows(source), columns(chunk)], h_rows.at[place_rows(2), columns(chunk)], second_side(chunk),
+                       ag_sems.at[0, 2, 0, chunk], ag_sems.at[0, 2, 1, chunk])
+
+    for chunk in range(col_chunks):
+        for start in range(chunk * BLOCK, (chunk + 1) * BLOCK, HEAD):
+            gain = gain_ref[:, start:start + HEAD].astype(F32)
+            h_rows[:quarter, start:start + HEAD] = (mid[:, start:start + HEAD] * scale * gain).astype(BF16)
+        gather_x(chunk).start()
+        gather_y(chunk).start()
+    for chunk in range(col_chunks):
+        (gather_x if chunk % 2 == 0 else gather_y)(chunk).wait_recv()
+        gather_cross(chunk).start()
+
+    for chunk in range(col_chunks):
+        (gather_y if chunk % 2 == 0 else gather_x)(chunk).wait_recv()
+        gather_cross(chunk).wait_recv()
+        for place, source in enumerate((own_half, peer_half)):
+            h_cols[columns(chunk), place * half:(place + 1) * half] = h_rows[source, columns(chunk)].astype(F32).T.astype(BF16)
+
+    def gu_copy(chunk):
+        slot = lax.rem(chunk, 4)
+        return to_core(gu_send.at[slot], gu_recv.at[slot], (gu_sems.at[0, slot], gu_sems.at[1, slot]))
+
+    def act_copy(chunk):
+        lanes = pl.ds(pl.multiple_of(chunk * BLOCK, BLOCK), BLOCK)
+        return to_core(act.at[own_half, lanes], act.at[own_half, lanes], (act_sems.at[0, chunk], act_sems.at[1, chunk]))
+
+    def ff_products(chunk):
+        slot = lax.rem(chunk, 4)
+        base = 2 * lax.rem(chunk, chunk_ring)
+        for kind in range(2):
+            product = jnp.dot(pool[slot_rows(base + kind), :], h_cols[...], preferred_element_type=F32)
+            gu_own[slot, kind] = product[:, :half]
+            gu_send[slot, kind] = product[:, half:].astype(BF16)
+
+    def activate(chunk):
+        slot = lax.rem(chunk, 4)
+        gate = gu_own[slot, 0] + gu_recv[slot, 0].astype(F32)
+        up = gu_own[slot, 1] + gu_recv[slot, 1].astype(F32)
+        value = gate * jax.nn.sigmoid(gate) * up
+        row = chunk * BLOCK + lax.broadcasted_iota(jnp.int32, value.shape, 0)
+        value = jnp.where(row < ff, value, 0.0)
+        lanes = pl.ds(pl.multiple_of(chunk * BLOCK, BLOCK), BLOCK)
+        act[own_half, lanes] = value.T.astype(BF16)
+
+    def refill(chunk):
+        ahead = chunk + chunk_ring
+        block = 2 * (ahead - ff_chunks)
+
+        @pl.when(ahead < ff_chunks - 1)
+        def _():
+            for copy in ff_copies(ahead):
+                copy.start()
+
+        @pl.when(ahead == ff_chunks - 1)
+        def _():
+            for copy in ff_copies(ahead, ff_rest):
+                copy.start()
+
+        @pl.when((ahead >= ff_chunks) & (block < ff_chunks - 1))
+        def _():
+            down_copy(block).start()
+            down_copy(block + 1).start()
+
+        @pl.when(block == ff_chunks - 1)
+        def _():
+            down_copy(block, ff_rest).start()
+
+    def ff_step(chunk, carry):
+        @pl.when(chunk >= 2)
+        def _():
+            gu_copy(chunk - 2).wait()
+        for copy in ff_copies(chunk):
+            copy.wait()
+
+        @pl.when(chunk >= 2)
+        def _():
+            activate(chunk - 2)
+            act_copy(chunk - 2).start()
+        ff_products(chunk)
+        gu_copy(chunk).start()
+        refill(chunk)
+        return carry
+
+    lax.fori_loop(0, ff_chunks - 1, ff_step, 0)
+    last = ff_chunks - 1
+    gu_copy(last - 2).wait()
+    for copy in ff_copies(last, ff_rest):
+        copy.wait()
+    activate(last - 2)
+    act_copy(last - 2).start()
+    ff_products(last)
+    gu_copy(last).start()
+
+    first_slot = (2 * ff_chunks) % RING
+    first_count = RING - first_slot
+    for block in range(first_count):
+        down_copy(block).wait()
+    split = first_count * BLOCK
+
+    def down_first(chunk):
+        return jnp.dot(act[:, :split], pool[first_slot * BLOCK:, columns(chunk)], preferred_element_type=F32)
+
+    def down_second(chunk):
+        return jnp.dot(act[:, split:], pool[:ff_chunks * BLOCK - split, columns(chunk)], preferred_element_type=F32)
+
+    for chunk in range(first_count):
+        act_copy(chunk).wait_recv()
+    early[0] = down_first(0)
+    gu_copy(last - 1).wait()
+    activate(last - 1)
+    act_copy(last - 1).start()
+    gu_copy(last).wait()
+    activate(last)
+    act_copy(last).start()
+    early[1] = down_first(1)
+    for block in range(first_count, ff_chunks):
+        down_copy(block, ff_rest if block == last else BLOCK).wait()
+    for chunk in range(first_count, ff_chunks):
+        act_copy(chunk).wait_recv()
+
+    def owner_rows(owner):
+        return pl.ds(pl.multiple_of(owner * quarter, quarter), quarter)
+
+    def final_x(chunk):
+        block = out_ref.at[owner_rows(my), columns(chunk)]
+        return to_chip(block, block, side_x, ag_sems.at[1, 0, 0, chunk], ag_sems.at[1, 0, 1, chunk])
+
+    def final_y(chunk):
+        block = out_ref.at[owner_rows(my), columns(chunk)]
+        return to_chip(block, block, side_y, ag_sems.at[1, 1, 0, chunk], ag_sems.at[1, 1, 1, chunk])
+
+    def final_cross(chunk):
+        block = out_ref.at[owner_rows(first_side(chunk)), columns(chunk)]
+        return to_chip(block, block, second_side(chunk), ag_sems.at[1, 2, 0, chunk], ag_sems.at[1, 2, 1, chunk])
+
+    def out_end(chunk):
+        out_ref[owner_rows(my), columns(chunk)] = (mid[:, columns(chunk)] + scatter_end(1, chunk)).astype(BF16)
+        final_x(chunk).start()
+        final_y(chunk).start()
+
+    def out_pass(chunk):
+        (final_x if chunk % 2 == 0 else final_y)(chunk).wait_recv()
+        final_cross(chunk).start()
+
+    for chunk in range(col_chunks + 9):
+        if chunk < col_chunks:
+            total = (early[chunk] if chunk < 2 else down_first(chunk)) + down_second(chunk)
+            scatter_start(1, chunk, total)
+        if 0 <= chunk - 3 < col_chunks:
+            scatter_pass(1, chunk - 3)
+        if 0 <= chunk - 6 < col_chunks:
+            out_end(chunk - 6)
+        if 0 <= chunk - 9 < col_chunks:
+            out_pass(chunk - 9)
+    for chunk in range(col_chunks):
+        (final_y if chunk % 2 == 0 else final_x)(chunk).wait_recv()
+        final_cross(chunk).wait()
+        final_x(chunk).wait_send()
+        final_y(chunk).wait_send()
+        gather_x(chunk).wait_send()
+        gather_y(chunk).wait_send()
+        gather_cross(chunk).wait_send()
+    for chunk in range(ff_chunks):
+        act_copy(chunk).wait_send()
+
+
+def tail(attn_rows, gain, x_in, w_o, wg_rows, wu_rows, w_down):
+    half, depth = attn_rows.shape
+    rows, hidden = x_in.shape
+    quarter = rows // 4
+    chunks = hidden // BLOCK
+    ff_chunks = pl.cdiv(w_down.shape[0], BLOCK)
+    return pl.pallas_call(
+        tail_kernel,
+        name="tail",
+        out_shape=jax.ShapeDtypeStruct((rows, hidden), BF16),
+        in_specs=vmem_specs(2) + any_specs(5),
+        out_specs=vmem_specs(1)[0],
+        scratch_shapes=[
+            VMEM((RING * BLOCK, hidden), BF16),
+            VMEM((rows, depth), BF16),
+            VMEM((rows, depth), BF16),
+            VMEM((chunks, 2 * quarter, BLOCK), BF16),
+            VMEM((chunks, 2, quarter, BLOCK), F32),
+            VMEM((chunks, 2 * quarter, BLOCK), BF16),
+            VMEM((chunks, quarter, BLOCK), BF16),
+            VMEM((chunks, quarter, BLOCK), BF16),
+            VMEM((quarter, hidden), BF16),
+            VMEM((quarter, hidden), F32),
+            VMEM((quarter, HEAD), F32),
+            VMEM((quarter, HEAD), F32),
+            VMEM((rows, hidden), BF16),
+            VMEM((hidden, rows), BF16),
+            VMEM((4, 2, BLOCK, half), BF16),
+            VMEM((4, 2, BLOCK, half), BF16),
+            VMEM((4, 2, BLOCK, half), F32),
+            VMEM((rows, ff_chunks * BLOCK), BF16),
+            VMEM((2, rows, BLOCK), F32),
+            DMA((RING,)),
+            DMA,
+            DMA((4,)),
+            DMA((2, 2, 2, chunks)),
+            DMA((2, 3, 2, chunks)),
+            DMA((2, 4)),
+            DMA((2, ff_chunks)),
+        ],
+        compiler_params=pltpu.CompilerParams(collective_id=1, has_side_effects=True, vmem_limit_bytes=67043328),
+    )(attn_rows, gain, x_in, w_o, wg_rows, wu_rows, w_down)
 
 
 def rotary_tables(positions):
@@ -252,33 +617,17 @@
 
 
 def solution(mesh):
-    mx_size = mesh.shape["mx"]
     act_spec = P(None, "mx")
     cache_spec = P("mx", None, "my", None)
     in_specs = (act_spec, P("mx"), P("mx"), P("mx"), P("mx", "my"), P("my"), P("mx", "my"), P("my"), P("mx", "my"), P("my"), P("my", "mx"), P("mx", "my"), P("mx", "my"), P("my", "mx"), cache_spec, cache_spec)
     out_specs = (act_spec, cache_spec, cache_spec)
 
     def local_layer(x_in, seq_lens, gain_attn, gain_mlp, w_q, b_q, w_k, b_k, w_v, b_v, w_o, w_gate, w_up, w_down, k_cache, v_cache):
-        hidden = x_in.shape[1] * mx_size
-        x_f32 = x_in.astype(F32)
         cos_tab, sin_tab = rotary_tables(seq_lens)
         bias = jnp.concatenate([b_q, b_k, b_v])[None, :]
         q_rot, kv_new = project(x_in, gain_attn[None, :], bias, cos_tab, sin_tab, w_q, w_k, w_v)
         attn_rows, k_cache_out, v_cache_out = attend(seq_lens, q_rot, kv_new, k_cache, v_cache)
-        attn_all = lax.all_gather(attn_rows, "mx", axis=0, tiled=True)
-        attn_proj = lax.psum(jnp.dot(attn_all, w_o, preferred_element_type=F32).astype(BF16), "my")
-        x_mid = (x_f32 + attn_proj.astype(F32)).astype(BF16)
-        mid_f32 = x_mid.astype(F32)
-        mlp_sq = lax.psum(jnp.sum(mid_f32 * mid_f32, axis=1, keepdims=True), "mx")
-        normed_mlp = (mid_f32 * lax.rsqrt(mlp_sq / hidden + NORM_EPS) * gain_mlp.astype(F32)).astype(BF16)
-        ff_cols = w_gate.shape[1]
-        gate_up = lax.psum(jnp.concatenate([
-            jnp.dot(normed_mlp, w_gate, preferred_element_type=F32).astype(BF16),
-            jnp.dot(normed_mlp, w_up, preferred_element_type=F32).astype(BF16),
-        ], axis=1), "mx").astype(F32)
-        hidden_act = (jax.nn.silu(gate_up[:, :ff_cols]) * gate_up[:, ff_cols:]).astype(BF16)
-        down_proj = lax.psum(jnp.dot(hidden_act, w_down, preferred_element_type=F32).astype(BF16), "my")
-        x_out = (mid_f32 + down_proj.astype(F32)).astype(BF16)
+        x_out = tail(attn_rows, gain_mlp[None, :], x_in, w_o, w_gate.T, w_up.T, w_down)
         return x_out, k_cache_out, v_cache_out
 
     return jax.shard_map(local_layer, mesh=mesh, in_specs=in_specs, out_specs=out_specs, check_vma=False)

time: 269 us -> 158 us (0.59)
  waiting for transfers between devices: 119 us -> 0 us
  Pallas kernels: 32.1 us -> 149 us
  matrix products: 56.8 us -> 0 us
  other arithmetic: 37.1 us -> 2.44 us
  between operations: 13.8 us -> 0.66 us
  blocking collectives: 4.92 us -> 0 us
    psum x3 -> x0, waiting for transfers between devices: 119 us -> none  [the longest x1 47.2 us: local_layer(): lax.psum(jnp.dot(attn_all, w_o, preferred_element_type=F32).astype(BF16),...]
    pallas_call x0 -> x1, Pallas kernels: none -> 115 us  [tail(): pl.pallas_call(tail_kernel, name='tail', out_shape=jax.ShapeDtypeStruct((...]
    dot_general x4 -> x0, matrix products: 56.8 us -> none  [the longest x1 20.7 us: local_layer(): jnp.dot(hidden_act, w_down, preferred_element_type=F32).astype(BF16)]
    concatenate x1 -> x0, other arithmetic: 22.7 us -> none  [local_layer(): jnp.concatenate([jnp.dot(normed_mlp, w_gate, preferred_element_type=F32)....]
    convert_element_type x3 -> x0, other arithmetic: 10.8 us -> none  [the longest x1 8.12 us: local_layer(): gate_up = lax.psum(jnp.concatenate([jnp.dot(normed_mlp, w_gate, preferred...]
  transfers between devices with their start and end apart: 3 -> 0, of which waited for: 3 -> 0; matrix products, arithmetic and copies ran while one was open for 0% -> 0% of each run, Pallas kernels for 0% -> 0%
where the time goes in v2:
time: 158 us
  Pallas kernels  149 us (94%)
  local copies, waits for them, and re-layouts  5.65 us (4%)
  other arithmetic  2.44 us (2%)
    pallas_call x1, Pallas kernels, tail(): pl.pallas_call(tail_kernel, name='tail', out_shape=jax.ShapeDtypeStruct((...  115 us
    pallas_call x1, Pallas kernels, attend(): pl.pallas_call(attend_kernel, name='attend', out_shape=(jax.ShapeDtypeStr...  25.2 us
    pallas_call x1, Pallas kernels, project(): pl.pallas_call(project_kernel, name='project', out_shape=(jax.ShapeDtypeS...  9.27 us

profile of v2, /device:TPU:0, one launch (start us, length us, event | category | flops | bytes accessed | tf_op | source)
XLA Modules:
  0.0 158.1 jit_solution(2494094531011603767)
XLA Ops:
  0.6 0.7 convert_element_type.3
  1.3 0.1 compare_select_fusion
  1.4 0.7 pad_maximum_fusion
  2.1 0.6 broadcast_in_dim.21.bias_ref
  2.7 1.3 broadcast_in_dim.20.gain_ref
  4.0 1.3 broadcast_in_dim.24.gain_ref
  5.3 1.0 fusion
  6.3 9.3 %project.1 = (bf16[128,1280]{1,0:T(8,128)(2,1)}, bf16[128,512]{1,0:T(8,128)(2,1)}) custom-call(bf16[256,2560]{1,0:T(8,128)(2,1)} %x_hbm.1, bf16[1,2560]{1,0:T(2,128)(2,1)} %broadcast_in_dim.20.gain_ref, bf16[1,1792]{1,0:T(2,128)(2,1)} %broadcast_in_dim.21.bias_ref, f32[128,128]{1,0:T(8,128)} %get-tuple-element.14.cos_ref, ...), custom_call_target="tpu_custom_call" | custom-call | tf_op jit(solution)/shard_map/project/pallas_call | solution.py:103
  15.5 25.2 %attend.1 = (bf16[128,1280]{1,0:T(8,128)(2,1)}, bf16[128,512,128]{2,1,0:T(8,128)(2,1)}, bf16[128,512,128]{2,1,0:T(8,128)(2,1)}) custom-call(s32[128]{0:T(128)} %lens_ref.1, bf16[128,1280]{1,0:T(8,128)(2,1)} %get-tuple-element.8.q_ref, bf16[128,512]{1,0:T(8,128)(2,1)} %get-tuple-element.9.kv_ref, bf16[128,512,128]{2,1,0:T(8,128)(2,1)} %bitcast.8, ...), custom_call_target="tpu_custom_call" | custom-call | tf_op jit(solution)/shard_map/attend/pallas_call | solution.py:221
  40.7 114.9 %tail.1 = bf16[256,2560]{1,0:T(8,128)(2,1)} custom-call(bf16[128,1280]{1,0:T(8,128)(2,1)} %get-tuple-element.10.attn_ref, bf16[1,2560]{1,0:T(2,128)(2,1)} %broadcast_in_dim.24.gain_ref, bf16[256,2560]{1,0:T(8,128)(2,1)} %x_hbm.1, bf16[1280,2560]{1,0:T(8,128)(2,1)} %wo_hbm.1, bf16[6848,2560]{1,0:T(8,128)(2,1)} %bitcast.6, bf16[6848,2560]{1,0:T(8,128)(2,1)} %bitcast.7, ...), custom_call_target="tpu_custom_call" | custom-call | tf_op jit(solution)/shard_map/tail/pallas_call | solution.py:573
  155.6 2.5 %copy.20 = bf16[256,2560]{1,0:T(8,128)(2,1)} copy(bf16[256,2560]{1,0:T(8,128)(2,1)} %tail.1) | data formatting | bytes 2621440
  (1 shorter events, 0.0 us)

commit v3 on v2

--- a/solution.py
+++ b/solution.py
@@ -1,5 +1,6 @@
 import jax
 import jax.numpy as jnp
+import numpy as np
 from jax import lax
 from jax.experimental import pallas as pl
 from jax.experimental.pallas import tpu as pltpu
@@ -24,8 +25,18 @@
     return [pl.BlockSpec(memory_space=pltpu.VMEM)] * count
 
 
-def project_kernel(x_ref, gain_ref, bias_ref, cos_ref, sin_ref, wq_hbm, wk_hbm, wv_hbm, q_out, kv_out,
-                   w_buf, normed, sq_send, sq_recv, part_send, part_recv, part_own, w_sems, send_sems, recv_sems):
+def lane_rows(vector):
+    return vector.reshape(-1, HEAD)
+
+
+def rotary_frequencies():
+    half_dim = HEAD // 2
+    inv_freq = np.float32(ROPE_THETA) ** (np.float32(-2.0) * np.arange(half_dim, dtype=np.float32) / np.float32(HEAD))
+    return jnp.asarray(np.concatenate([inv_freq, inv_freq])[None, :], F32)
+
+
+def project_kernel(gain_ref, bq_ref, bk_ref, bv_ref, lens_ref, freq_ref, x_hbm, wq_hbm, wk_hbm, wv_hbm, q_out, kv_out,
+                   x_ref, x_sem, w_buf, normed, sq_send, sq_recv, part_send, part_recv, part_own, w_sems, send_sems, recv_sems):
     me = lax.axis_index("mx")
     peer = 1 - me
     rows, depth = x_ref.shape
@@ -41,11 +52,20 @@
             source = (wk_hbm, wv_hbm)[index - q_chunks]
         return pltpu.make_async_copy(source, w_buf.at[index], w_sems.at[index])
 
+    x_copy = pltpu.make_async_copy(x_hbm, x_ref, x_sem)
+    x_copy.start()
     for index in range(chunks):
         weight_copy(index).start()
     barrier = pltpu.get_barrier_semaphore()
     pl.semaphore_signal(barrier, inc=1, device_id={"mx": peer}, device_id_type=MESH)
 
+    positions = jnp.broadcast_to(lens_ref[...].astype(F32), (half, half)).T
+    angles = positions * freq_ref[...]
+    cos_tab = jnp.cos(angles)
+    lane = lax.broadcasted_iota(jnp.int32, (half, HEAD), 1)
+    sin_tab = jnp.where(lane < HEAD // 2, -1.0, 1.0) * jnp.sin(angles)
+
+    x_copy.wait()
     total = jnp.zeros((rows, HEAD), F32)
     for start in range(0, depth, HEAD):
         block = x_ref[:, start:start + HEAD].astype(F32)
@@ -63,9 +83,10 @@
     sq_copy.start()
     sq_copy.wait()
     scale = lax.rsqrt((sq_send[...] + sq_recv[...]) / (2 * depth) + NORM_EPS)
+    gains = gain_ref[...].astype(F32)
     for start in range(0, depth, HEAD):
         block = x_ref[:, start:start + HEAD].astype(F32)
-        gain = gain_ref[:, start:start + HEAD].astype(F32)
+        gain = gains[start // HEAD:start // HEAD + 1, :]
         normed[:, start:start + HEAD] = (block * scale * gain).astype(BF16)
 
     own_rows = pl.ds(pl.multiple_of(me * half, half), half)
@@ -79,14 +100,17 @@
         copies.append(remote(part_send.at[index], part_recv.at[index], index))
         copies[index].start()
 
-    cos_tab = cos_ref[...]
-    sin_tab = sin_ref[...]
+    biases = [ref[...].astype(F32) for ref in (bq_ref, bk_ref, bv_ref)]
     for index in range(chunks):
         copies[index].wait()
         for head in range(2):
             lanes = slice(head * HEAD, (head + 1) * HEAD)
             columns = slice(index * width + head * HEAD, index * width + (head + 1) * HEAD)
-            value = part_own[index][:, lanes] + part_recv[index][:, lanes].astype(F32) + bias_ref[:, columns].astype(F32)
+            if index < q_chunks:
+                bias = biases[0][2 * index + head:2 * index + head + 1, :]
+            else:
+                bias = biases[index - q_chunks + 1][head:head + 1, :]
+            value = part_own[index][:, lanes] + part_recv[index][:, lanes].astype(F32) + bias
             if index < chunks - 1:
                 value = value * cos_tab + pltpu.roll(value, HEAD // 2, 1) * sin_tab
             if index < q_chunks:
@@ -95,7 +119,7 @@
                 kv_out[:, (index - q_chunks) * width + head * HEAD:(index - q_chunks) * width + (head + 1) * HEAD] = value.astype(BF16)
 
 
-def project(x_in, gain, bias, cos_tab, sin_tab, w_q, w_k, w_v):
+def project(x_in, seq_lens, gain, b_q, b_k, b_v, w_q, w_k, w_v):
     rows, depth = x_in.shape
     half = rows // 2
     width = 2 * HEAD
@@ -104,9 +128,11 @@
         project_kernel,
         name="project",
         out_shape=(jax.ShapeDtypeStruct((half, w_q.shape[1]), BF16), jax.ShapeDtypeStruct((half, 2 * width), BF16)),
-        in_specs=vmem_specs(5) + any_specs(3),
+        in_specs=vmem_specs(6) + any_specs(4),
         out_specs=tuple(vmem_specs(2)),
         scratch_shapes=[
+            VMEM((rows, depth), BF16),
+            DMA,
             VMEM((chunks, depth, width), BF16),
             VMEM((rows, depth), BF16),
             VMEM((rows, HEAD), F32),
@@ -119,7 +145,7 @@
             DMA((chunks + 1,)),
         ],
         compiler_params=pltpu.CompilerParams(collective_id=0, has_side_effects=True, vmem_limit_bytes=67043328),
-    )(x_in, gain, bias, cos_tab, sin_tab, w_q, w_k, w_v)
+    )(lane_rows(gain), lane_rows(b_q), lane_rows(b_k), lane_rows(b_v), seq_lens[None, :], rotary_frequencies(), x_in, w_q, w_k, w_v)
 
 
 SLOTS = 4
@@ -247,17 +273,17 @@
 RING = 36
 
 
-def tail_kernel(attn_ref, gain_ref, x_hbm, wo_hbm, wg_hbm, wu_hbm, wd_hbm, out_ref,
-                pool, full, rows_in, part, keep, recv_one, send_two, recv_two, x_own, mid, sq_send, sq_recv,
+def tail_kernel(gain_ref, attn_hbm, x_hbm, wo_hbm, wg_hbm, wu_hbm, wd_hbm, out_hbm,
+                out_ref, out_sems, pool, full, rows_in, part, keep, recv_one, send_two, recv_two, x_own, mid, sq_send, sq_recv,
                 h_rows, h_cols, gu_send, gu_recv, gu_own, act, early,
-                pool_sems, x_sem, core_sems, rs_sems, ag_sems, gu_sems, act_sems):
+                pool_sems, x_sem, attn_sem, core_sems, rs_sems, ag_sems, gu_sems, act_sems):
     my = lax.axis_index("my")
     me = lax.axis_index("mx")
     peer = 1 - me
     side_x = my + 1 - 2 * lax.rem(my, 2)
     side_y = lax.rem(my + 2, 4)
     cross = 3 - my
-    half, depth = attn_ref.shape
+    half, depth = attn_hbm.shape
     batch = 2 * half
     quarter = batch // 4
     hidden = x_hbm.shape[1]
@@ -293,14 +319,15 @@
         return pltpu.make_async_remote_copy(src_ref=source, dst_ref=target, send_sem=send_sem, recv_sem=recv_sem,
                                             device_id={"my": chip}, device_id_type=MESH)
 
+    own_half = pl.ds(pl.multiple_of(me * half, half), half)
+    peer_half = pl.ds(pl.multiple_of(peer * half, half), half)
+    attn_load = pltpu.make_async_copy(attn_hbm, full.at[own_half], attn_sem)
+    attn_load.start()
     for block in range(out_blocks):
         out_copy(block).start()
     own_rows = pl.ds(pl.multiple_of(my * quarter, quarter), quarter)
     x_copy = pltpu.make_async_copy(x_hbm.at[own_rows], x_own, x_sem)
     x_copy.start()
-    for chunk in range(out_slot // 2):
-        for copy in ff_copies(chunk):
-            copy.start()
 
     barrier = pltpu.get_barrier_semaphore()
     pl.semaphore_signal(barrier, inc=1, device_id={"mx": peer}, device_id_type=MESH)
@@ -308,11 +335,9 @@
     pl.semaphore_signal(barrier, inc=1, device_id={"my": side_y}, device_id_type=MESH)
     pl.semaphore_wait(barrier, 3)
 
-    own_half = pl.ds(pl.multiple_of(me * half, half), half)
-    peer_half = pl.ds(pl.multiple_of(peer * half, half), half)
-    attn_copy = to_core(attn_ref, full.at[own_half], (core_sems.at[0], core_sems.at[1]))
+    attn_load.wait()
+    attn_copy = to_core(full.at[own_half], full.at[own_half], (core_sems.at[0], core_sems.at[1]))
     attn_copy.start()
-    full[own_half, :] = attn_ref[...]
     attn_copy.wait()
     for place, owner in enumerate((my, side_x, cross, side_y)):
         rows_in[place * quarter:(place + 1) * quarter, :] = full[pl.ds(pl.multiple_of(owner * quarter, quarter), quarter), :]
@@ -360,6 +385,9 @@
     x_copy.wait()
     for block in range(out_blocks):
         out_copy(block).wait()
+    for chunk in range(out_slot // 2):
+        for copy in ff_copies(chunk):
+            copy.start()
     for chunk in range(col_chunks):
         weights = pool[out_slot * BLOCK:out_slot * BLOCK + depth, columns(chunk)]
         scatter_start(0, chunk, jnp.dot(rows_in[...], weights, preferred_element_type=F32))
@@ -400,9 +428,10 @@
         return to_chip(h_rows.at[place_rows(source), columns(chunk)], h_rows.at[place_rows(2), columns(chunk)], second_side(chunk),
                        ag_sems.at[0, 2, 0, chunk], ag_sems.at[0, 2, 1, chunk])
 
+    gains = gain_ref[...].astype(F32)
     for chunk in range(col_chunks):
         for start in range(chunk * BLOCK, (chunk + 1) * BLOCK, HEAD):
-            gain = gain_ref[:, start:start + HEAD].astype(F32)
+            gain = gains[start // HEAD:start // HEAD + 1, :]
             h_rows[:quarter, start:start + HEAD] = (mid[:, start:start + HEAD] * scale * gain).astype(BF16)
         gather_x(chunk).start()
         gather_y(chunk).start()
@@ -427,10 +456,11 @@
     def ff_products(chunk):
         slot = lax.rem(chunk, 4)
         base = 2 * lax.rem(chunk, chunk_ring)
+        product = jnp.dot(pool[slot_rows(base, 2 * BLOCK), :], h_cols[...], preferred_element_type=F32)
         for kind in range(2):
-            product = jnp.dot(pool[slot_rows(base + kind), :], h_cols[...], preferred_element_type=F32)
-            gu_own[slot, kind] = product[:, :half]
-            gu_send[slot, kind] = product[:, half:].astype(BF16)
+            rows = slice(kind * BLOCK, (kind + 1) * BLOCK)
+            gu_own[slot, kind] = product[rows, :half]
+            gu_send[slot, kind] = product[rows, half:].astype(BF16)
 
     def activate(chunk):
         slot = lax.rem(chunk, 4)
@@ -466,22 +496,23 @@
             down_copy(block, ff_rest).start()
 
     def ff_step(chunk, carry):
-        @pl.when(chunk >= 2)
-        def _():
-            gu_copy(chunk - 2).wait()
+        gu_copy(chunk - 2).wait()
         for copy in ff_copies(chunk):
             copy.wait()
-
-        @pl.when(chunk >= 2)
-        def _():
-            activate(chunk - 2)
-            act_copy(chunk - 2).start()
+        activate(chunk - 2)
+        ff_products(chunk)
+        gu_copy(chunk).start()
+        act_copy(chunk - 2).start()
+        refill(chunk)
+        return carry
+
+    for chunk in range(2):
+        for copy in ff_copies(chunk):
+            copy.wait()
         ff_products(chunk)
         gu_copy(chunk).start()
         refill(chunk)
-        return carry
-
-    lax.fori_loop(0, ff_chunks - 1, ff_step, 0)
+    lax.fori_loop(2, ff_chunks - 1, ff_step, 0)
     last = ff_chunks - 1
     gu_copy(last - 2).wait()
     for copy in ff_copies(last, ff_rest):
@@ -533,6 +564,9 @@
         block = out_ref.at[owner_rows(first_side(chunk)), columns(chunk)]
         return to_chip(block, block, second_side(chunk), ag_sems.at[1, 2, 0, chunk], ag_sems.at[1, 2, 1, chunk])
 
+    def save_out(chunk):
+        return pltpu.make_async_copy(out_ref.at[:, columns(chunk)], out_hbm.at[:, columns(chunk)], out_sems.at[chunk])
+
     def out_end(chunk):
         out_ref[owner_rows(my), columns(chunk)] = (mid[:, columns(chunk)] + scatter_end(1, chunk)).astype(BF16)
         final_x(chunk).start()
@@ -554,12 +588,16 @@
             out_pass(chunk - 9)
     for chunk in range(col_chunks):
         (final_y if chunk % 2 == 0 else final_x)(chunk).wait_recv()
-        final_cross(chunk).wait()
+        final_cross(chunk).wait_recv()
+        save_out(chunk).start()
+    for chunk in range(col_chunks):
+        final_cross(chunk).wait_send()
         final_x(chunk).wait_send()
         final_y(chunk).wait_send()
         gather_x(chunk).wait_send()
         gather_y(chunk).wait_send()
         gather_cross(chunk).wait_send()
+        save_out(chunk).wait()
     for chunk in range(ff_chunks):
         act_copy(chunk).wait_send()
 
@@ -574,9 +612,11 @@
         tail_kernel,
         name="tail",
         out_shape=jax.ShapeDtypeStruct((rows, hidden), BF16),
-        in_specs=vmem_specs(2) + any_specs(5),
-        out_specs=vmem_specs(1)[0],
+        in_specs=vmem_specs(1) + any_specs(6),
+        out_specs=any_specs(1)[0],
         scratch_shapes=[
+            VMEM((rows, hidden), BF16),
+            DMA((chunks,)),
             VMEM((RING * BLOCK, hidden), BF16),
             VMEM((rows, depth), BF16),
             VMEM((rows, depth), BF16),
@@ -598,6 +638,7 @@
             VMEM((2, rows, BLOCK), F32),
             DMA((RING,)),
             DMA,
+            DMA,
             DMA((4,)),
             DMA((2, 2, 2, chunks)),
             DMA((2, 3, 2, chunks)),
@@ -605,15 +646,7 @@
             DMA((2, ff_chunks)),
         ],
         compiler_params=pltpu.CompilerParams(collective_id=1, has_side_effects=True, vmem_limit_bytes=67043328),
-    )(attn_rows, gain, x_in, w_o, wg_rows, wu_rows, w_down)
-
-
-def rotary_tables(positions):
-    half_dim = HEAD // 2
-    inv_freq = ROPE_THETA ** (-2.0 * jnp.arange(half_dim, dtype=F32) / HEAD)
-    angles = positions.astype(F32)[:, None] * jnp.concatenate([inv_freq, inv_freq])
-    sign = jnp.where(jnp.arange(HEAD) < half_dim, -1.0, 1.0)
-    return jnp.cos(angles), jnp.sin(angles) * sign
+    )(lane_rows(gain), attn_rows, x_in, w_o, wg_rows, wu_rows, w_down)
 
 
 def solution(mesh):
@@ -623,11 +656,9 @@
     out_specs = (act_spec, cache_spec, cache_spec)
 
     def local_layer(x_in, seq_lens, gain_attn, gain_mlp, w_q, b_q, w_k, b_k, w_v, b_v, w_o, w_gate, w_up, w_down, k_cache, v_cache):
-        cos_tab, sin_tab = rotary_tables(seq_lens)
-        bias = jnp.concatenate([b_q, b_k, b_v])[None, :]
-        q_rot, kv_new = project(x_in, gain_attn[None, :], bias, cos_tab, sin_tab, w_q, w_k, w_v)
+        q_rot, kv_new = project(x_in, seq_lens, gain_attn, b_q, b_k, b_v, w_q, w_k, w_v)
         attn_rows, k_cache_out, v_cache_out = attend(seq_lens, q_rot, kv_new, k_cache, v_cache)
-        x_out = tail(attn_rows, gain_mlp[None, :], x_in, w_o, w_gate.T, w_up.T, w_down)
+        x_out = tail(attn_rows, gain_mlp, x_in, w_o, w_gate.T, w_up.T, w_down)
         return x_out, k_cache_out, v_cache_out
 
     return jax.shard_map(local_layer, mesh=mesh, in_specs=in_specs, out_specs=out_specs, check_vma=False)

time: 158 us -> 145 us (0.918)
  Pallas kernels: 149 us -> 142 us
  local copies, waits for them, and re-layouts: 5.65 us -> 2.46 us
  other arithmetic: 2.44 us -> 0 us
    pallas_call x1, Pallas kernels: 115 us -> 104 us  [tail(): pl.pallas_call(tail_kernel, name='tail', out_shape=jax.ShapeDtypeStruct((...]
    broadcast_in_dim x3 -> x0, local copies, waits for them, and re-layouts: 3.19 us -> none  [the longest x1 1.3 us: local_layer(): gain_attn[None, :]]
    pallas_call x1, Pallas kernels: 9.27 us -> 12.3 us  [project(): pl.pallas_call(project_kernel, name='project', out_shape=(jax.ShapeDtypeS...]
where the time goes in v3:
time: 145 us
  Pallas kernels  142 us (98%)
  local copies, waits for them, and re-layouts  2.46 us (2%)
    pallas_call x1, Pallas kernels, tail(): pl.pallas_call(tail_kernel, name='tail', out_shape=jax.ShapeDtypeStruct((...  104 us
    pallas_call x1, Pallas kernels, attend(): pl.pallas_call(attend_kernel, name='attend', out_shape=(jax.ShapeDtypeStr...  25.2 us
    pallas_call x1, Pallas kernels, project(): pl.pallas_call(project_kernel, name='project', out_shape=(jax.ShapeDtypeS...  12.3 us

profile of v3, /device:TPU:0, one launch (start us, length us, event | category | flops | bytes accessed | tf_op | source)
XLA Modules:
  0.0 144.8 jit_solution(9714006609761215170)
XLA Ops:
  0.6 12.3 %project.1 = (bf16[128,1280]{1,0:T(8,128)(2,1)}, bf16[128,512]{1,0:T(8,128)(2,1)}) custom-call(bf16[20,128]{1,0:T(8,128)(2,1)} %bitcast.16, bf16[10,128]{1,0:T(8,128)(2,1)} %bitcast.18, bf16[2,128]{1,0:T(2,128)(2,1)} %bitcast.20, bf16[2,128]{1,0:T(2,128)(2,1)} %bitcast.21, s32[1,128]{1,0:T(1,128)} %bitcast.19, f32[1,128]{1,0:T(1,128)} %constant.2.clone.freq_ref, ...), custom_call_target="tpu_custom_call" | custom-call | tf_op jit(solution)/shard_map/project/pallas_call | solution.py:127
  13.0 25.2 %attend.1 = (bf16[128,1280]{1,0:T(8,128)(2,1)}, bf16[128,512,128]{2,1,0:T(8,128)(2,1)}, bf16[128,512,128]{2,1,0:T(8,128)(2,1)}) custom-call(s32[128]{0:T(128)} %lens_ref.1, bf16[128,1280]{1,0:T(8,128)(2,1)} %get-tuple-element.8.q_ref, bf16[128,512]{1,0:T(8,128)(2,1)} %get-tuple-element.9.kv_ref, bf16[128,512,128]{2,1,0:T(8,128)(2,1)} %bitcast.14, ...), custom_call_target="tpu_custom_call" | custom-call | tf_op jit(solution)/shard_map/attend/pallas_call | solution.py:247
  38.2 104.1 %tail.1 = bf16[256,2560]{1,0:T(8,128)(2,1)} custom-call(bf16[20,128]{1,0:T(8,128)(2,1)} %bitcast.17, bf16[128,1280]{1,0:T(8,128)(2,1)} %get-tuple-element.10.attn_hbm, bf16[256,2560]{1,0:T(8,128)(2,1)} %x_hbm.3, bf16[1280,2560]{1,0:T(8,128)(2,1)} %wo_hbm.1, bf16[6848,2560]{1,0:T(8,128)(2,1)} %bitcast.12, bf16[6848,2560]{1,0:T(8,128)(2,1)} %bitcast.13, ...), custom_call_target="tpu_custom_call" | custom-call | tf_op jit(solution)/shard_map/tail/pallas_call | solution.py:611
  142.3 2.5 %copy.21 = bf16[256,2560]{1,0:T(8,128)(2,1)} copy(bf16[256,2560]{1,0:T(8,128)(2,1)} %tail.1) | data formatting | bytes 2621440

commit v4 on v3

--- a/solution.py
+++ b/solution.py
@@ -52,10 +52,11 @@
             source = (wk_hbm, wv_hbm)[index - q_chunks]
         return pltpu.make_async_copy(source, w_buf.at[index], w_sems.at[index])
 
+    def weight_wait(index):
+        pltpu.make_async_copy(wk_hbm, w_buf.at[index], w_sems.at[index]).wait()
+
     x_copy = pltpu.make_async_copy(x_hbm, x_ref, x_sem)
     x_copy.start()
-    for index in range(chunks):
-        weight_copy(index).start()
     barrier = pltpu.get_barrier_semaphore()
     pl.semaphore_signal(barrier, inc=1, device_id={"mx": peer}, device_id_type=MESH)
 
@@ -66,6 +67,8 @@
     sin_tab = jnp.where(lane < HEAD // 2, -1.0, 1.0) * jnp.sin(angles)
 
     x_copy.wait()
+    for index in range(chunks):
+        weight_copy(index).start()
     total = jnp.zeros((rows, HEAD), F32)
     for start in range(0, depth, HEAD):
         block = x_ref[:, start:start + HEAD].astype(F32)
@@ -82,27 +85,32 @@
     sq_copy = remote(sq_send, sq_recv, chunks)
     sq_copy.start()
     sq_copy.wait()
+    own_rows = pl.ds(pl.multiple_of(me * half, half), half)
+    peer_rows = pl.ds(pl.multiple_of(peer * half, half), half)
     scale = lax.rsqrt((sq_send[...] + sq_recv[...]) / (2 * depth) + NORM_EPS)
     gains = gain_ref[...].astype(F32)
     for start in range(0, depth, HEAD):
         block = x_ref[:, start:start + HEAD].astype(F32)
         gain = gains[start // HEAD:start // HEAD + 1, :]
-        normed[:, start:start + HEAD] = (block * scale * gain).astype(BF16)
-
-    own_rows = pl.ds(pl.multiple_of(me * half, half), half)
-    peer_rows = pl.ds(pl.multiple_of(peer * half, half), half)
-    copies = []
-    for index in range(chunks):
-        weight_copy(index).wait()
-        weights = w_buf.at[index]
-        part_send[index] = jnp.dot(normed[peer_rows, :], weights[...], preferred_element_type=F32).astype(BF16)
-        part_own[index] = jnp.dot(normed[own_rows, :], weights[...], preferred_element_type=F32)
-        copies.append(remote(part_send.at[index], part_recv.at[index], index))
-        copies[index].start()
-
+        value = (block * scale * gain).astype(BF16)
+        normed[own_rows, start:start + HEAD] = value[:half]
+        normed[peer_rows, start:start + HEAD] = value[half:]
+
+    def part_copy(index):
+        return remote(part_send.at[index], part_recv.at[index], index)
+
+    def multiply(index, carry):
+        weight_wait(index)
+        product = jnp.dot(normed[...], w_buf[index], preferred_element_type=F32)
+        part_own[index] = product[:half]
+        part_send[index] = product[half:].astype(BF16)
+        part_copy(index).start()
+        return carry
+
+    lax.fori_loop(0, chunks, multiply, 0)
     biases = [ref[...].astype(F32) for ref in (bq_ref, bk_ref, bv_ref)]
     for index in range(chunks):
-        copies[index].wait()
+        part_copy(index).wait()
         for head in range(2):
             lanes = slice(head * HEAD, (head + 1) * HEAD)
             columns = slice(index * width + head * HEAD, index * width + (head + 1) * HEAD)
@@ -274,7 +282,7 @@
 
 
 def tail_kernel(gain_ref, attn_hbm, x_hbm, wo_hbm, wg_hbm, wu_hbm, wd_hbm, out_hbm,
-                out_ref, out_sems, pool, full, rows_in, part, keep, recv_one, send_two, recv_two, x_own, mid, sq_send, sq_recv,
+                out_ref, pool, full, rows_in, part, keep, recv_one, send_two, recv_two, x_own, mid, sq_send, sq_recv,
                 h_rows, h_cols, gu_send, gu_recv, gu_own, act, early,
                 pool_sems, x_sem, attn_sem, core_sems, rs_sems, ag_sems, gu_sems, act_sems):
     my = lax.axis_index("my")
@@ -294,6 +302,10 @@
     chunk_ring = RING // 2
     out_blocks = depth // BLOCK
     out_slot = RING - 6
+    down_slot = RING - ff_chunks
+    early_blocks = chunk_ring
+    late_chunk = chunk_ring + chunk_ring // 2 - (down_slot // 2)
+    late_count = ff_chunks - late_chunk
 
     def slot_rows(slot, count=BLOCK):
         return pl.ds(pl.multiple_of(slot * BLOCK, BLOCK), count)
@@ -301,12 +313,16 @@
     def block_copy(source, block, slot, count=BLOCK):
         return pltpu.make_async_copy(source.at[slot_rows(block, count)], pool.at[slot_rows(slot, count)], pool_sems.at[slot])
 
+    def ff_slot(chunk):
+        return 2 * jnp.where(chunk < chunk_ring, chunk, jnp.where(chunk < late_chunk, chunk - late_chunk + chunk_ring // 2, chunk - late_chunk))
+
     def ff_copies(chunk, count=BLOCK):
-        slot = 2 * lax.rem(chunk, chunk_ring)
+        slot = ff_slot(chunk)
         return block_copy(wg_hbm, chunk, slot, count), block_copy(wu_hbm, chunk, slot + 1, count)
 
     def down_copy(block, count=BLOCK):
-        return block_copy(wd_hbm, block, lax.rem(2 * ff_chunks + block, RING), count)
+        slot = down_slot + jnp.where(block < early_blocks, block + ff_chunks - early_blocks, block - early_blocks)
+        return block_copy(wd_hbm, block, slot, count)
 
     def out_copy(block):
         return block_copy(wo_hbm, block, out_slot + block)
@@ -323,8 +339,6 @@
     peer_half = pl.ds(pl.multiple_of(peer * half, half), half)
     attn_load = pltpu.make_async_copy(attn_hbm, full.at[own_half], attn_sem)
     attn_load.start()
-    for block in range(out_blocks):
-        out_copy(block).start()
     own_rows = pl.ds(pl.multiple_of(my * quarter, quarter), quarter)
     x_copy = pltpu.make_async_copy(x_hbm.at[own_rows], x_own, x_sem)
     x_copy.start()
@@ -333,9 +347,10 @@
     pl.semaphore_signal(barrier, inc=1, device_id={"mx": peer}, device_id_type=MESH)
     pl.semaphore_signal(barrier, inc=1, device_id={"my": side_x}, device_id_type=MESH)
     pl.semaphore_signal(barrier, inc=1, device_id={"my": side_y}, device_id_type=MESH)
+    attn_load.wait()
+    for block in range(out_blocks):
+        out_copy(block).start()
     pl.semaphore_wait(barrier, 3)
-
-    attn_load.wait()
     attn_copy = to_core(full.at[own_half], full.at[own_half], (core_sems.at[0], core_sems.at[1]))
     attn_copy.start()
     attn_copy.wait()
@@ -343,44 +358,48 @@
         rows_in[place * quarter:(place + 1) * quarter, :] = full[pl.ds(pl.multiple_of(owner * quarter, quarter), quarter), :]
 
     def columns(chunk):
-        return slice(chunk * BLOCK, (chunk + 1) * BLOCK)
-
-    def first_side(chunk):
-        return (side_x, side_y)[chunk % 2]
-
-    def second_side(chunk):
-        return (side_y, side_x)[chunk % 2]
-
-    def scatter_one(stage, chunk):
-        sems = rs_sems.at[stage, 0]
-        return to_chip(part.at[chunk], recv_one.at[chunk], first_side(chunk), sems.at[0, chunk], sems.at[1, chunk])
-
-    def scatter_two(stage, chunk):
-        sems = rs_sems.at[stage, 1]
-        return to_chip(send_two.at[chunk], recv_two.at[chunk], second_side(chunk), sems.at[0, chunk], sems.at[1, chunk])
-
-    def scatter_start(stage, chunk, total):
-        lead = quarter * (1 + chunk % 2)
-        part[chunk] = total[lead:lead + 2 * quarter].astype(BF16)
-        keep[chunk, 0] = total[:quarter]
-        other = 3 * quarter if chunk % 2 == 0 else quarter
-        keep[chunk, 1] = total[other:other + quarter]
-        scatter_one(stage, chunk).start()
-
-    def scatter_pass(stage, chunk):
-        scatter_one(stage, chunk).wait()
-        mine = slice(0, quarter) if chunk % 2 == 0 else slice(quarter, 2 * quarter)
-        theirs = slice(quarter, 2 * quarter) if chunk % 2 == 0 else slice(0, quarter)
+        if isinstance(chunk, int):
+            return slice(chunk * BLOCK, (chunk + 1) * BLOCK)
+        return pl.ds(pl.multiple_of(chunk * BLOCK, BLOCK), BLOCK)
+
+    def first_side(parity):
+        return (side_x, side_y)[parity]
+
+    def second_side(parity):
+        return (side_y, side_x)[parity]
+
+    def scatter_one(chunk, parity):
+        return to_chip(part.at[chunk], recv_one.at[chunk], first_side(parity), rs_sems.at[0, 0, chunk], rs_sems.at[0, 1, chunk])
+
+    def scatter_two(chunk, parity):
+        return to_chip(send_two.at[chunk], recv_two.at[chunk], second_side(parity), rs_sems.at[1, 0, chunk], rs_sems.at[1, 1, chunk])
+
+    def scatter_start(pair, total):
+        for parity in range(2):
+            chunk = 2 * pair + parity
+            value = total[:, parity * BLOCK:(parity + 1) * BLOCK]
+            lead = quarter * (1 + parity)
+            part[chunk] = value[lead:lead + 2 * quarter].astype(BF16)
+            keep[chunk, 0] = value[:quarter]
+            other = 3 * quarter if parity == 0 else quarter
+            keep[chunk, 1] = value[other:other + quarter]
+        for parity in range(2):
+            scatter_one(2 * pair + parity, parity).start()
+
+    def scatter_pass(chunk, parity):
+        scatter_one(chunk, parity).wait()
+        mine = slice(0, quarter) if parity == 0 else slice(quarter, 2 * quarter)
+        theirs = slice(quarter, 2 * quarter) if parity == 0 else slice(0, quarter)
         send_two[chunk] = (keep[chunk, 1] + recv_one[chunk, theirs, :].astype(F32)).astype(BF16)
-        scatter_two(stage, chunk).start()
+        scatter_two(chunk, parity).start()
         keep[chunk, 0] = keep[chunk, 0] + recv_one[chunk, mine, :].astype(F32)
 
-    def scatter_end(stage, chunk):
-        scatter_two(stage, chunk).wait()
+    def scatter_end(chunk, parity):
+        scatter_two(chunk, parity).wait()
         return keep[chunk, 0] + recv_two[chunk].astype(F32)
 
     def mid_end(chunk):
-        mid[:, columns(chunk)] = (x_own[:, columns(chunk)].astype(F32) + scatter_end(0, chunk)).astype(BF16).astype(F32)
+        mid[:, columns(chunk)] = (x_own[:, columns(chunk)].astype(F32) + scatter_end(chunk, chunk % 2)).astype(BF16).astype(F32)
 
     x_copy.wait()
     for block in range(out_blocks):
@@ -388,20 +407,21 @@
     for chunk in range(out_slot // 2):
         for copy in ff_copies(chunk):
             copy.start()
-    for chunk in range(col_chunks):
-        weights = pool[out_slot * BLOCK:out_slot * BLOCK + depth, columns(chunk)]
-        scatter_start(0, chunk, jnp.dot(rows_in[...], weights, preferred_element_type=F32))
-        if chunk >= 3:
-            scatter_pass(0, chunk - 3)
-        if chunk >= 7:
-            mid_end(chunk - 7)
+    def out_product(pair, carry):
+        lanes = pl.ds(pl.multiple_of(pair * 2 * BLOCK, 2 * BLOCK), 2 * BLOCK)
+        weights = pool[out_slot * BLOCK:out_slot * BLOCK + depth, lanes]
+        scatter_start(pair, jnp.dot(rows_in[...], weights, preferred_element_type=F32))
+        return carry
+
+    lax.fori_loop(0, col_chunks // 2, out_product, 0)
     for chunk in range(out_slot // 2, chunk_ring):
         for copy in ff_copies(chunk):
             copy.start()
-    for chunk in range(col_chunks, col_chunks + 7):
-        if chunk - 3 < col_chunks:
-            scatter_pass(0, chunk - 3)
-        mid_end(chunk - 7)
+    for chunk in range(col_chunks + 3):
+        if chunk < col_chunks:
+            scatter_pass(chunk, chunk % 2)
+        if chunk >= 3:
+            mid_end(chunk - 3)
 
     square = jnp.zeros((quarter, HEAD), F32)
     for start in range(0, hidden, HEAD):
@@ -417,16 +437,16 @@
 
     def gather_x(chunk):
         return to_chip(h_rows.at[place_rows(0), columns(chunk)], h_rows.at[place_rows(1), columns(chunk)], side_x,
-                       ag_sems.at[0, 0, 0, chunk], ag_sems.at[0, 0, 1, chunk])
+                       ag_sems.at[0, 0, chunk], ag_sems.at[0, 1, chunk])
 
     def gather_y(chunk):
         return to_chip(h_rows.at[place_rows(0), columns(chunk)], h_rows.at[place_rows(3), columns(chunk)], side_y,
-                       ag_sems.at[0, 1, 0, chunk], ag_sems.at[0, 1, 1, chunk])
+                       ag_sems.at[1, 0, chunk], ag_sems.at[1, 1, chunk])
 
     def gather_cross(chunk):
         source = 1 if chunk % 2 == 0 else 3
-        return to_chip(h_rows.at[place_rows(source), columns(chunk)], h_rows.at[place_rows(2), columns(chunk)], second_side(chunk),
-                       ag_sems.at[0, 2, 0, chunk], ag_sems.at[0, 2, 1, chunk])
+        return to_chip(h_rows.at[place_rows(source), columns(chunk)], h_rows.at[place_rows(2), columns(chunk)], second_side(chunk % 2),
+                       ag_sems.at[2, 0, chunk], ag_sems.at[2, 1, chunk])
 
     gains = gain_ref[...].astype(F32)
     for chunk in range(col_chunks):
@@ -444,18 +464,25 @@
         gather_cross(chunk).wait_recv()
         for place, source in enumerate((own_half, peer_half)):
             h_cols[columns(chunk), place * half:(place + 1) * half] = h_rows[source, columns(chunk)].astype(F32).T.astype(BF16)
+        gather_x(chunk).wait_send()
+        gather_y(chunk).wait_send()
+        gather_cross(chunk).wait_send()
 
     def gu_copy(chunk):
         slot = lax.rem(chunk, 4)
         return to_core(gu_send.at[slot], gu_recv.at[slot], (gu_sems.at[0, slot], gu_sems.at[1, slot]))
 
+    def act_lanes(chunk):
+        place = jnp.where(chunk < early_blocks, chunk + ff_chunks - early_blocks, chunk - early_blocks)
+        return pl.ds(pl.multiple_of(place * BLOCK, BLOCK), BLOCK)
+
     def act_copy(chunk):
-        lanes = pl.ds(pl.multiple_of(chunk * BLOCK, BLOCK), BLOCK)
-        return to_core(act.at[own_half, lanes], act.at[own_half, lanes], (act_sems.at[0, chunk], act_sems.at[1, chunk]))
+        lanes = act_lanes(chunk)
+        return to_core(act.at[own_half, lanes], act.at[own_half, lanes], (act_sems.at[0, lax.rem(chunk, 8)], act_sems.at[1, lax.rem(chunk, 8)]))
 
     def ff_products(chunk):
         slot = lax.rem(chunk, 4)
-        base = 2 * lax.rem(chunk, chunk_ring)
+        base = ff_slot(chunk)
         product = jnp.dot(pool[slot_rows(base, 2 * BLOCK), :], h_cols[...], preferred_element_type=F32)
         for kind in range(2):
             rows = slice(kind * BLOCK, (kind + 1) * BLOCK)
@@ -469,33 +496,50 @@
         value = gate * jax.nn.sigmoid(gate) * up
         row = chunk * BLOCK + lax.broadcasted_iota(jnp.int32, value.shape, 0)
         value = jnp.where(row < ff, value, 0.0)
-        lanes = pl.ds(pl.multiple_of(chunk * BLOCK, BLOCK), BLOCK)
+        lanes = act_lanes(chunk)
         act[own_half, lanes] = value.T.astype(BF16)
 
     def refill(chunk):
-        ahead = chunk + chunk_ring
-        block = 2 * (ahead - ff_chunks)
-
-        @pl.when(ahead < ff_chunks - 1)
-        def _():
-            for copy in ff_copies(ahead):
+        half_ring = chunk_ring // 2
+
+        @pl.when(chunk < late_count - 1)
+        def _():
+            for copy in ff_copies(late_chunk + chunk):
                 copy.start()
 
-        @pl.when(ahead == ff_chunks - 1)
-        def _():
-            for copy in ff_copies(ahead, ff_rest):
+        @pl.when(chunk == late_count - 1)
+        def _():
+            for copy in ff_copies(ff_chunks - 1, ff_rest):
                 copy.start()
 
-        @pl.when((ahead >= ff_chunks) & (block < ff_chunks - 1))
-        def _():
-            down_copy(block).start()
-            down_copy(block + 1).start()
-
-        @pl.when(block == ff_chunks - 1)
-        def _():
-            down_copy(block, ff_rest).start()
+        @pl.when((chunk >= late_count) & (chunk < half_ring))
+        def _():
+            for copy in ff_copies(chunk - late_count + chunk_ring):
+                copy.start()
+
+        @pl.when((chunk >= half_ring) & (chunk < chunk_ring))
+        def _():
+            down_copy(2 * (chunk - half_ring)).start()
+            down_copy(2 * (chunk - half_ring) + 1).start()
+
+        free = 2 * (chunk - chunk_ring + late_count) - down_slot + early_blocks
+
+        @pl.when((chunk >= chunk_ring) & (chunk < late_chunk) & (free >= early_blocks))
+        def _():
+            down_copy(free).start()
+
+        @pl.when((chunk >= chunk_ring) & (chunk < late_chunk - 1))
+        def _():
+            down_copy(free + 1).start()
+
+        @pl.when(chunk == late_chunk - 1)
+        def _():
+            down_copy(ff_chunks - 1, ff_rest).start()
 
     def ff_step(chunk, carry):
+        @pl.when(chunk >= 7)
+        def _():
+            act_copy(chunk - 7).wait()
         gu_copy(chunk - 2).wait()
         for copy in ff_copies(chunk):
             copy.wait()
@@ -506,69 +550,73 @@
         refill(chunk)
         return carry
 
-    for chunk in range(2):
+    def ff_first(chunk, carry):
         for copy in ff_copies(chunk):
             copy.wait()
         ff_products(chunk)
         gu_copy(chunk).start()
         refill(chunk)
+        return carry
+
+    lax.fori_loop(0, 2, ff_first, 0)
     lax.fori_loop(2, ff_chunks - 1, ff_step, 0)
     last = ff_chunks - 1
+    act_copy(last - 7).wait()
     gu_copy(last - 2).wait()
     for copy in ff_copies(last, ff_rest):
         copy.wait()
     activate(last - 2)
-    act_copy(last - 2).start()
     ff_products(last)
     gu_copy(last).start()
-
-    first_slot = (2 * ff_chunks) % RING
-    first_count = RING - first_slot
-    for block in range(first_count):
+    act_copy(last - 2).start()
+
+    for block in range(early_blocks):
         down_copy(block).wait()
-    split = first_count * BLOCK
-
-    def down_first(chunk):
-        return jnp.dot(act[:, :split], pool[first_slot * BLOCK:, columns(chunk)], preferred_element_type=F32)
-
-    def down_second(chunk):
-        return jnp.dot(act[:, split:], pool[:ff_chunks * BLOCK - split, columns(chunk)], preferred_element_type=F32)
-
-    for chunk in range(first_count):
-        act_copy(chunk).wait_recv()
-    early[0] = down_first(0)
+    late_lanes = (ff_chunks - early_blocks) * BLOCK
+    late_row = down_slot * BLOCK + late_lanes
+
+    def pair_lanes(pair):
+        return pl.ds(pl.multiple_of(pair * 2 * BLOCK, 2 * BLOCK), 2 * BLOCK)
+
+    for chunk in range(last - 6, last - 3):
+        act_copy(chunk).wait()
+
+    def down_early(pair, carry):
+        early[...] = jnp.dot(act[:, late_lanes:], pool[late_row:, pair_lanes(pair)], preferred_element_type=F32)
+        return carry
+
+    lax.fori_loop(0, 1, down_early, 0)
     gu_copy(last - 1).wait()
     activate(last - 1)
     act_copy(last - 1).start()
     gu_copy(last).wait()
     activate(last)
     act_copy(last).start()
-    early[1] = down_first(1)
-    for block in range(first_count, ff_chunks):
+    for block in range(early_blocks, ff_chunks):
         down_copy(block, ff_rest if block == last else BLOCK).wait()
-    for chunk in range(first_count, ff_chunks):
-        act_copy(chunk).wait_recv()
+    for chunk in range(last - 3, ff_chunks):
+        act_copy(chunk).wait()
 
     def owner_rows(owner):
         return pl.ds(pl.multiple_of(owner * quarter, quarter), quarter)
 
     def final_x(chunk):
         block = out_ref.at[owner_rows(my), columns(chunk)]
-        return to_chip(block, block, side_x, ag_sems.at[1, 0, 0, chunk], ag_sems.at[1, 0, 1, chunk])
+        return to_chip(block, block, side_x, ag_sems.at[0, 0, chunk], ag_sems.at[0, 1, chunk])
 
     def final_y(chunk):
         block = out_ref.at[owner_rows(my), columns(chunk)]
-        return to_chip(block, block, side_y, ag_sems.at[1, 1, 0, chunk], ag_sems.at[1, 1, 1, chunk])
+        return to_chip(block, block, side_y, ag_sems.at[1, 0, chunk], ag_sems.at[1, 1, chunk])
 
     def final_cross(chunk):
-        block = out_ref.at[owner_rows(first_side(chunk)), columns(chunk)]
-        return to_chip(block, block, second_side(chunk), ag_sems.at[1, 2, 0, chunk], ag_sems.at[1, 2, 1, chunk])
+        block = out_ref.at[owner_rows(first_side(chunk % 2)), columns(chunk)]
+        return to_chip(block, block, second_side(chunk % 2), ag_sems.at[2, 0, chunk], ag_sems.at[2, 1, chunk])
 
     def save_out(chunk):
-        return pltpu.make_async_copy(out_ref.at[:, columns(chunk)], out_hbm.at[:, columns(chunk)], out_sems.at[chunk])
+        return pltpu.make_async_copy(out_ref.at[:, columns(chunk)], out_hbm.at[:, columns(chunk)], pool_sems.at[chunk])
 
     def out_end(chunk):
-        out_ref[owner_rows(my), columns(chunk)] = (mid[:, columns(chunk)] + scatter_end(1, chunk)).astype(BF16)
+        out_ref[owner_rows(my), columns(chunk)] = (mid[:, columns(chunk)] + scatter_end(chunk, chunk % 2)).astype(BF16)
         final_x(chunk).start()
         final_y(chunk).start()
 
@@ -576,16 +624,37 @@
         (final_x if chunk % 2 == 0 else final_y)(chunk).wait_recv()
         final_cross(chunk).start()
 
-    for chunk in range(col_chunks + 9):
-        if chunk < col_chunks:
-            total = (early[chunk] if chunk < 2 else down_first(chunk)) + down_second(chunk)
-            scatter_start(1, chunk, total)
-        if 0 <= chunk - 3 < col_chunks:
-            scatter_pass(1, chunk - 3)
-        if 0 <= chunk - 6 < col_chunks:
-            out_end(chunk - 6)
-        if 0 <= chunk - 9 < col_chunks:
-            out_pass(chunk - 9)
+    def down_rest(pair, carry):
+        total = jnp.dot(act[:, :late_lanes], pool[down_slot * BLOCK:late_row, pair_lanes(pair)], preferred_element_type=F32)
+        scatter_start(pair, early[...] + total)
+        return carry
+
+    def down_pair(pair, carry):
+        scatter_start(pair, jnp.dot(act[...], pool[down_slot * BLOCK:, pair_lanes(pair)], preferred_element_type=F32))
+
+        @pl.when(pair >= 2)
+        def _():
+            for parity in range(2):
+                scatter_pass(2 * (pair - 2) + parity, parity)
+        return carry
+
+    pairs = col_chunks // 2
+    lax.fori_loop(0, 1, down_rest, 0)
+    lax.fori_loop(1, pairs, down_pair, 0)
+    passed = 2 * (pairs - 2)
+    for step in range(passed, col_chunks + 6):
+        if step < col_chunks:
+            scatter_pass(step, step % 2)
+        if step == passed:
+            for chunk in range(passed - 2):
+                out_end(chunk)
+        if 0 <= step - 2 < col_chunks and step - 2 >= passed - 2:
+            out_end(step - 2)
+        if step == passed:
+            for chunk in range(passed - 4):
+                out_pass(chunk)
+        if 0 <= step - 4 < col_chunks and step - 4 >= passed - 4:
+            out_pass(step - 4)
     for chunk in range(col_chunks):
         (final_y if chunk % 2 == 0 else final_x)(chunk).wait_recv()
         final_cross(chunk).wait_recv()
@@ -594,12 +663,7 @@
         final_cross(chunk).wait_send()
         final_x(chunk).wait_send()
         final_y(chunk).wait_send()
-        gather_x(chunk).wait_send()
-        gather_y(chunk).wait_send()
-        gather_cross(chunk).wait_send()
         save_out(chunk).wait()
-    for chunk in range(ff_chunks):
-        act_copy(chunk).wait_send()
 
 
 def tail(attn_rows, gain, x_in, w_o, wg_rows, wu_rows, w_down):
@@ -616,7 +680,6 @@
         out_specs=any_specs(1)[0],
         scratch_shapes=[
             VMEM((rows, hidden), BF16),
-            DMA((chunks,)),
             VMEM((RING * BLOCK, hidden), BF16),
             VMEM((rows, depth), BF16),
             VMEM((rows, depth), BF16),
@@ -635,15 +698,15 @@
             VMEM((4, 2, BLOCK, half), BF16),
             VMEM((4, 2, BLOCK, half), F32),
             VMEM((rows, ff_chunks * BLOCK), BF16),
-            VMEM((2, rows, BLOCK), F32),
+            VMEM((rows, 2 * BLOCK), F32),
             DMA((RING,)),
             DMA,
             DMA,
             DMA((4,)),
-            DMA((2, 2, 2, chunks)),
-            DMA((2, 3, 2, chunks)),
+            DMA((2, 2, chunks)),
+            DMA((3, 2, chunks)),
             DMA((2, 4)),
-            DMA((2, ff_chunks)),
+            DMA((2, 8)),
         ],
         compiler_params=pltpu.CompilerParams(collective_id=1, has_side_effects=True, vmem_limit_bytes=67043328),
     )(lane_rows(gain), attn_rows, x_in, w_o, wg_rows, wu_rows, w_down)

time: 145 us -> 136 us (0.938)
  Pallas kernels: 142 us -> 133 us
    pallas_call x1, Pallas kernels: 104 us -> 97.9 us  [tail(): pl.pallas_call(tail_kernel, name='tail', out_shape=jax.ShapeDtypeStruct((...]
    pallas_call x1, Pallas kernels: 12.3 us -> 9.89 us  [project(): pl.pallas_call(project_kernel, name='project', out_shape=(jax.ShapeDtypeS...]
where the time goes in v4:
time: 136 us
  Pallas kernels  133 us (98%)
  local copies, waits for them, and re-layouts  2.46 us (2%)
    pallas_call x1, Pallas kernels, tail(): pl.pallas_call(tail_kernel, name='tail', out_shape=jax.ShapeDtypeStruct((...  97.9 us
    pallas_call x1, Pallas kernels, attend(): pl.pallas_call(attend_kernel, name='attend', out_shape=(jax.ShapeDtypeStr...  25.2 us
    pallas_call x1, Pallas kernels, project(): pl.pallas_call(project_kernel, name='project', out_shape=(jax.ShapeDtypeS...  9.89 us

profile of v4, /device:TPU:0, one launch (start us, length us, event | category | flops | bytes accessed | tf_op | source)
XLA Modules:
  0.0 136.1 jit_solution(1720128674177106192)
XLA Ops:
  0.6 9.9 %project.1 = (bf16[128,1280]{1,0:T(8,128)(2,1)}, bf16[128,512]{1,0:T(8,128)(2,1)}) custom-call(bf16[20,128]{1,0:T(8,128)(2,1)} %bitcast.16, bf16[10,128]{1,0:T(8,128)(2,1)} %bitcast.18, bf16[2,128]{1,0:T(2,128)(2,1)} %bitcast.20, bf16[2,128]{1,0:T(2,128)(2,1)} %bitcast.21, s32[1,128]{1,0:T(1,128)} %bitcast.19, f32[1,128]{1,0:T(1,128)} %constant.2.clone.freq_ref, ...), custom_call_target="tpu_custom_call" | custom-call | tf_op jit(solution)/shard_map/project/pallas_call | solution.py:135
  10.5 25.2 %attend.1 = (bf16[128,1280]{1,0:T(8,128)(2,1)}, bf16[128,512,128]{2,1,0:T(8,128)(2,1)}, bf16[128,512,128]{2,1,0:T(8,128)(2,1)}) custom-call(s32[128]{0:T(128)} %lens_ref.1, bf16[128,1280]{1,0:T(8,128)(2,1)} %get-tuple-element.8.q_ref, bf16[128,512]{1,0:T(8,128)(2,1)} %get-tuple-element.9.kv_ref, bf16[128,512,128]{2,1,0:T(8,128)(2,1)} %bitcast.14, ...), custom_call_target="tpu_custom_call" | custom-call | tf_op jit(solution)/shard_map/attend/pallas_call | solution.py:255
  35.7 97.9 %tail.1 = bf16[256,2560]{1,0:T(8,128)(2,1)} custom-call(bf16[20,128]{1,0:T(8,128)(2,1)} %bitcast.17, bf16[128,1280]{1,0:T(8,128)(2,1)} %get-tuple-element.10.attn_hbm, bf16[256,2560]{1,0:T(8,128)(2,1)} %x_hbm.3, bf16[1280,2560]{1,0:T(8,128)(2,1)} %wo_hbm.1, bf16[6848,2560]{1,0:T(8,128)(2,1)} %bitcast.12, bf16[6848,2560]{1,0:T(8,128)(2,1)} %bitcast.13, ...), custom_call_target="tpu_custom_call" | custom-call | tf_op jit(solution)/shard_map/tail/pallas_call | solution.py:675
  133.6 2.5 %copy.21 = bf16[256,2560]{1,0:T(8,128)(2,1)} copy(bf16[256,2560]{1,0:T(8,128)(2,1)} %tail.1) | data formatting | bytes 2621440

commit v5 on v4

--- a/solution.py
+++ b/solution.py
@@ -35,11 +35,11 @@
     return jnp.asarray(np.concatenate([inv_freq, inv_freq])[None, :], F32)
 
 
-def project_kernel(gain_ref, bq_ref, bk_ref, bv_ref, lens_ref, freq_ref, x_hbm, wq_hbm, wk_hbm, wv_hbm, q_out, kv_out,
-                   x_ref, x_sem, w_buf, normed, sq_send, sq_recv, part_send, part_recv, part_own, w_sems, send_sems, recv_sems):
+def project_kernel(gain_hbm, bq_hbm, bk_hbm, bv_hbm, lens_hbm, freq_hbm, x_hbm, wq_hbm, wk_hbm, wv_hbm, q_out, kv_out,
+                   gain_ref, bq_ref, bk_ref, bv_ref, lens_ref, freq_ref, small_sems, x_ref, x_sem, w_buf, normed, sq_send, sq_recv, part_send, part_recv, part_own, w_sems, send_sems, recv_sems):
     me = lax.axis_index("mx")
     peer = 1 - me
-    rows, depth = x_ref.shape
+    rows, depth = x_hbm.shape
     half = rows // 2
     width = 2 * HEAD
     q_chunks = wq_hbm.shape[1] // width
@@ -55,11 +55,17 @@
     def weight_wait(index):
         pltpu.make_async_copy(wk_hbm, w_buf.at[index], w_sems.at[index]).wait()
 
+    smalls = [pltpu.make_async_copy(source, target, small_sems.at[slot]) for slot, (source, target) in enumerate((
+        (lens_hbm, lens_ref), (freq_hbm, freq_ref), (gain_hbm, gain_ref), (bq_hbm, bq_ref), (bk_hbm, bk_ref), (bv_hbm, bv_ref)))]
+    for copy in smalls:
+        copy.start()
     x_copy = pltpu.make_async_copy(x_hbm, x_ref, x_sem)
     x_copy.start()
     barrier = pltpu.get_barrier_semaphore()
     pl.semaphore_signal(barrier, inc=1, device_id={"mx": peer}, device_id_type=MESH)
 
+    for copy in smalls:
+        copy.wait()
     positions = jnp.broadcast_to(lens_ref[...].astype(F32), (half, half)).T
     angles = positions * freq_ref[...]
     cos_tab = jnp.cos(angles)
@@ -136,9 +142,16 @@
         project_kernel,
         name="project",
         out_shape=(jax.ShapeDtypeStruct((half, w_q.shape[1]), BF16), jax.ShapeDtypeStruct((half, 2 * width), BF16)),
-        in_specs=vmem_specs(6) + any_specs(4),
+        in_specs=any_specs(10),
         out_specs=tuple(vmem_specs(2)),
         scratch_shapes=[
+            VMEM((depth // HEAD, HEAD), BF16),
+            VMEM((w_q.shape[1] // HEAD, HEAD), BF16),
+            VMEM((2, HEAD), BF16),
+            VMEM((2, HEAD), BF16),
+            VMEM((1, half), jnp.int32),
+            VMEM((1, HEAD), F32),
+            DMA((6,)),
             VMEM((rows, depth), BF16),
             DMA,
             VMEM((chunks, depth, width), BF16),
@@ -156,14 +169,14 @@
     )(lane_rows(gain), lane_rows(b_q), lane_rows(b_k), lane_rows(b_v), seq_lens[None, :], rotary_frequencies(), x_in, w_q, w_k, w_v)
 
 
-SLOTS = 4
+SLOTS = 6
 ROWS_STEP = 8
 
 
-def attend_kernel(lens_ref, q_ref, kv_ref, k_hbm, v_hbm, o_ref, k_out, v_out,
-                  k_buf, v_buf, q_wide, q_packed, kv_wide, o_wide, parity, scores, weights, sums, in_sems, out_sems):
+def attend_kernel(lens_ref, q_hbm, kv_hbm, k_hbm, v_hbm, o_ref, k_out, v_out,
+                  q_ref, kv_ref, small_sems, k_buf, v_buf, q_wide, q_packed, kv_wide, o_wide, parity, scores, weights, sums, in_sems, out_sems):
     batch, kv_rows, _ = k_hbm.shape
-    q_heads = q_ref.shape[1] // HEAD
+    q_heads = q_hbm.shape[1] // HEAD
     group = q_heads // 2
     steps = batch // ROWS_STEP
 
@@ -177,11 +190,17 @@
         source, target = ((k_buf, k_out), (v_buf, v_out))[kind]
         return pltpu.make_async_copy(source.at[slot], target.at[pl.ds(step * ROWS_STEP, ROWS_STEP)], out_sems.at[kind, slot])
 
-    for step in range(2):
+    q_copy = pltpu.make_async_copy(q_hbm, q_ref, small_sems.at[0])
+    kv_copy = pltpu.make_async_copy(kv_hbm, kv_ref, small_sems.at[1])
+    q_copy.start()
+    kv_copy.start()
+    for step in range(3):
         for kind in range(2):
             load(step, kind).start()
 
     q_wide[...] = jnp.zeros_like(q_wide)
+    q_copy.wait()
+    kv_copy.wait()
     for head in range(q_heads):
         q_wide[pl.ds(head, batch, stride=QPAD), :] = q_ref[:, head * HEAD:(head + 1) * HEAD].astype(F32)
     q_packed[...] = q_wide[...].astype(BF16)
@@ -200,14 +219,14 @@
     def body(step, carry):
         slot = lax.rem(step, SLOTS)
 
-        @pl.when(step + 2 < steps)
-        def _():
-            @pl.when(step >= 2)
+        @pl.when(step + 3 < steps)
+        def _():
+            @pl.when(step >= 3)
             def _():
                 for kind in range(2):
-                    save(step - 2, kind).wait()
+                    save(step - 3, kind).wait()
             for kind in range(2):
-                load(step + 2, kind).start()
+                load(step + 3, kind).start()
 
         for kind in range(2):
             load(step, kind).wait()
@@ -256,9 +275,12 @@
         attend_kernel,
         name="attend",
         out_shape=(jax.ShapeDtypeStruct(q_rot.shape, BF16), jax.ShapeDtypeStruct(flat, BF16), jax.ShapeDtypeStruct(flat, BF16)),
-        in_specs=[pl.BlockSpec(memory_space=pltpu.SMEM)] + vmem_specs(2) + any_specs(2),
+        in_specs=[pl.BlockSpec(memory_space=pltpu.SMEM)] + any_specs(4),
         out_specs=tuple(vmem_specs(1) + any_specs(2)),
         scratch_shapes=[
+            VMEM(q_rot.shape, BF16),
+            VMEM(kv_new.shape, BF16),
+            DMA((2,)),
             VMEM((SLOTS, ROWS_STEP, rows, HEAD), BF16),
             VMEM((SLOTS, ROWS_STEP, rows, HEAD), BF16),
             VMEM((batch * QPAD, HEAD), F32),
@@ -281,8 +303,8 @@
 RING = 36
 
 
-def tail_kernel(gain_ref, attn_hbm, x_hbm, wo_hbm, wg_hbm, wu_hbm, wd_hbm, out_hbm,
-                out_ref, pool, full, rows_in, part, keep, recv_one, send_two, recv_two, x_own, mid, sq_send, sq_recv,
+def tail_kernel(gain_hbm, attn_hbm, x_hbm, wo_hbm, wg_hbm, wu_hbm, wd_hbm, out_hbm,
+                out_ref, gain_ref, gain_sem, pool, full, rows_in, part, keep, recv_one, send_two, recv_two, x_own, mid, sq_send, sq_recv,
                 h_rows, h_cols, gu_send, gu_recv, gu_own, act, early,
                 pool_sems, x_sem, attn_sem, core_sems, rs_sems, ag_sems, gu_sems, act_sems):
     my = lax.axis_index("my")
@@ -342,6 +364,8 @@
     own_rows = pl.ds(pl.multiple_of(my * quarter, quarter), quarter)
     x_copy = pltpu.make_async_copy(x_hbm.at[own_rows], x_own, x_sem)
     x_copy.start()
+    gain_copy = pltpu.make_async_copy(gain_hbm, gain_ref, gain_sem)
+    gain_copy.start()
 
     barrier = pltpu.get_barrier_semaphore()
     pl.semaphore_signal(barrier, inc=1, device_id={"mx": peer}, device_id_type=MESH)
@@ -402,6 +426,7 @@
         mid[:, columns(chunk)] = (x_own[:, columns(chunk)].astype(F32) + scatter_end(chunk, chunk % 2)).astype(BF16).astype(F32)
 
     x_copy.wait()
+    gain_copy.wait()
     for block in range(out_blocks):
         out_copy(block).wait()
     for chunk in range(out_slot // 2):
@@ -469,7 +494,7 @@
         gather_cross(chunk).wait_send()
 
     def gu_copy(chunk):
-        slot = lax.rem(chunk, 4)
+        slot = lax.rem(chunk, 8)
         return to_core(gu_send.at[slot], gu_recv.at[slot], (gu_sems.at[0, slot], gu_sems.at[1, slot]))
 
     def act_lanes(chunk):
@@ -481,7 +506,7 @@
         return to_core(act.at[own_half, lanes], act.at[own_half, lanes], (act_sems.at[0, lax.rem(chunk, 8)], act_sems.at[1, lax.rem(chunk, 8)]))
 
     def ff_products(chunk):
-        slot = lax.rem(chunk, 4)
+        slot = lax.rem(chunk, 8)
         base = ff_slot(chunk)
         product = jnp.dot(pool[slot_rows(base, 2 * BLOCK), :], h_cols[...], preferred_element_type=F32)
         for kind in range(2):
@@ -490,7 +515,7 @@
             gu_send[slot, kind] = product[rows, half:].astype(BF16)
 
     def activate(chunk):
-        slot = lax.rem(chunk, 4)
+        slot = lax.rem(chunk, 8)
         gate = gu_own[slot, 0] + gu_recv[slot, 0].astype(F32)
         up = gu_own[slot, 1] + gu_recv[slot, 1].astype(F32)
         value = gate * jax.nn.sigmoid(gate) * up
@@ -536,40 +561,62 @@
         def _():
             down_copy(ff_chunks - 1, ff_rest).start()
 
-    def ff_step(chunk, carry):
-        @pl.when(chunk >= 7)
-        def _():
-            act_copy(chunk - 7).wait()
-        gu_copy(chunk - 2).wait()
-        for copy in ff_copies(chunk):
-            copy.wait()
-        activate(chunk - 2)
-        ff_products(chunk)
-        gu_copy(chunk).start()
-        act_copy(chunk - 2).start()
-        refill(chunk)
-        return carry
-
-    def ff_first(chunk, carry):
-        for copy in ff_copies(chunk):
+    def ff_pair(pair, active):
+        chunks = (2 * pair, 2 * pair + 1)
+        if active:
+            for chunk in chunks:
+                gu_copy(chunk - 4).wait()
+        for chunk in chunks:
+            for copy in ff_copies(chunk):
+                copy.wait()
+        if active:
+            for chunk in chunks:
+                activate(chunk - 4)
+        for chunk in chunks:
+            ff_products(chunk)
+        for chunk in chunks:
+            gu_copy(chunk).start()
+        if active:
+            for chunk in chunks:
+                act_copy(chunk - 4).start()
+        for chunk in chunks:
+            refill(chunk)
+
+    def ff_first(pair, carry):
+        ff_pair(pair, False)
+        return carry
+
+    def ff_step(pair, carry):
+        @pl.when(pair >= 4)
+        def _():
+            for parity in range(2):
+                act_copy(2 * (pair - 4) + parity).wait()
+        ff_pair(pair, True)
+        return carry
+
+    last = ff_chunks - 1
+    ff_pairs = last // 2
+    lax.fori_loop(0, 2, ff_first, 0)
+    lax.fori_loop(2, ff_pairs, ff_step, 0)
+
+    def finish(chunk):
+        gu_copy(chunk).wait()
+        activate(chunk)
+        act_copy(chunk).start()
+
+    for chunk in range(2 * ff_pairs - 8, 2 * ff_pairs - 6):
+        act_copy(chunk).wait()
+
+    def ff_last(chunk, carry):
+        for copy in ff_copies(chunk, ff_rest):
             copy.wait()
         ff_products(chunk)
         gu_copy(chunk).start()
-        refill(chunk)
-        return carry
-
-    lax.fori_loop(0, 2, ff_first, 0)
-    lax.fori_loop(2, ff_chunks - 1, ff_step, 0)
-    last = ff_chunks - 1
-    act_copy(last - 7).wait()
-    gu_copy(last - 2).wait()
-    for copy in ff_copies(last, ff_rest):
-        copy.wait()
-    activate(last - 2)
-    ff_products(last)
-    gu_copy(last).start()
-    act_copy(last - 2).start()
-
+        return carry
+
+    lax.fori_loop(last, last + 1, ff_last, 0)
+    for chunk in range(last - 4, last - 2):
+        finish(chunk)
     for block in range(early_blocks):
         down_copy(block).wait()
     late_lanes = (ff_chunks - early_blocks) * BLOCK
@@ -578,23 +625,17 @@
     def pair_lanes(pair):
         return pl.ds(pl.multiple_of(pair * 2 * BLOCK, 2 * BLOCK), 2 * BLOCK)
 
-    for chunk in range(last - 6, last - 3):
-        act_copy(chunk).wait()
-
     def down_early(pair, carry):
-        early[...] = jnp.dot(act[:, late_lanes:], pool[late_row:, pair_lanes(pair)], preferred_element_type=F32)
+        early[pair] = jnp.dot(act[:, late_lanes:], pool[late_row:, pair_lanes(pair)], preferred_element_type=F32)
         return carry
 
     lax.fori_loop(0, 1, down_early, 0)
-    gu_copy(last - 1).wait()
-    activate(last - 1)
-    act_copy(last - 1).start()
-    gu_copy(last).wait()
-    activate(last)
-    act_copy(last).start()
+    for chunk in range(last - 2, ff_chunks):
+        finish(chunk)
+    lax.fori_loop(1, 2, down_early, 0)
     for block in range(early_blocks, ff_chunks):
         down_copy(block, ff_rest if block == last else BLOCK).wait()
-    for chunk in range(last - 3, ff_chunks):
+    for chunk in range(2 * ff_pairs - 6, ff_chunks):
         act_copy(chunk).wait()
 
     def owner_rows(owner):
@@ -626,7 +667,7 @@
 
     def down_rest(pair, carry):
         total = jnp.dot(act[:, :late_lanes], pool[down_slot * BLOCK:late_row, pair_lanes(pair)], preferred_element_type=F32)
-        scatter_start(pair, early[...] + total)
+        scatter_start(pair, early[pair] + total)
         return carry
 
     def down_pair(pair, carry):
@@ -639,22 +680,26 @@
         return carry
 
     pairs = col_chunks // 2
-    lax.fori_loop(0, 1, down_rest, 0)
-    lax.fori_loop(1, pairs, down_pair, 0)
-    passed = 2 * (pairs - 2)
-    for step in range(passed, col_chunks + 6):
-        if step < col_chunks:
-            scatter_pass(step, step % 2)
-        if step == passed:
-            for chunk in range(passed - 2):
-                out_end(chunk)
-        if 0 <= step - 2 < col_chunks and step - 2 >= passed - 2:
-            out_end(step - 2)
-        if step == passed:
-            for chunk in range(passed - 4):
-                out_pass(chunk)
-        if 0 <= step - 4 < col_chunks and step - 4 >= passed - 4:
-            out_pass(step - 4)
+    lax.fori_loop(0, 2, down_rest, 0)
+    lax.fori_loop(2, pairs, down_pair, 0)
+
+    def each(step, pair):
+        for chunk in (2 * pair, 2 * pair + 1):
+            if step is scatter_pass:
+                step(chunk, chunk % 2)
+            else:
+                step(chunk)
+
+    each(out_end, 0)
+    for pair in range(pairs - 2, pairs):
+        each(scatter_pass, pair)
+        each(out_end, pair - pairs + 3)
+    each(out_pass, 0)
+    for pair in range(3, pairs):
+        each(out_end, pair)
+        each(out_pass, pair - 2)
+    for pair in range(pairs - 2, pairs):
+        each(out_pass, pair)
     for chunk in range(col_chunks):
         (final_y if chunk % 2 == 0 else final_x)(chunk).wait_recv()
         final_cross(chunk).wait_recv()
@@ -676,10 +721,12 @@
         tail_kernel,
         name="tail",
         out_shape=jax.ShapeDtypeStruct((rows, hidden), BF16),
-        in_specs=vmem_specs(1) + any_specs(6),
+        in_specs=any_specs(7),
         out_specs=any_specs(1)[0],
         scratch_shapes=[
             VMEM((rows, hidden), BF16),
+            VMEM((hidden // HEAD, HEAD), BF16),
+            DMA,
             VMEM((RING * BLOCK, hidden), BF16),
             VMEM((rows, depth), BF16),
             VMEM((rows, depth), BF16),
@@ -694,18 +741,18 @@
             VMEM((quarter, HEAD), F32),
             VMEM((rows, hidden), BF16),
             VMEM((hidden, rows), BF16),
-            VMEM((4, 2, BLOCK, half), BF16),
-            VMEM((4, 2, BLOCK, half), BF16),
-            VMEM((4, 2, BLOCK, half), F32),
+            VMEM((8, 2, BLOCK, half), BF16),
+            VMEM((8, 2, BLOCK, half), BF16),
+            VMEM((8, 2, BLOCK, half), F32),
             VMEM((rows, ff_chunks * BLOCK), BF16),
-            VMEM((rows, 2 * BLOCK), F32),
+            VMEM((2, rows, 2 * BLOCK), F32),
             DMA((RING,)),
             DMA,
             DMA,
             DMA((4,)),
             DMA((2, 2, chunks)),
             DMA((3, 2, chunks)),
-            DMA((2, 4)),
+            DMA((2, 8)),
             DMA((2, 8)),
         ],
         compiler_params=pltpu.CompilerParams(collective_id=1, has_side_effects=True, vmem_limit_bytes=67043328),

time: 136 us -> 130 us (0.956)
  Pallas kernels: 133 us -> 127 us
    pallas_call x1, Pallas kernels: 97.9 us -> 91.7 us  [tail(): pl.pallas_call(tail_kernel, name='tail', out_shape=jax.ShapeDtypeStruct((...]
where the time goes in v5:
time: 130 us
  Pallas kernels  127 us (98%)
  local copies, waits for them, and re-layouts  2.46 us (2%)
    pallas_call x1, Pallas kernels, tail(): pl.pallas_call(tail_kernel, name='tail', out_shape=jax.ShapeDtypeStruct((...  91.7 us
    pallas_call x1, Pallas kernels, attend(): pl.pallas_call(attend_kernel, name='attend', out_shape=(jax.ShapeDtypeStr...  25.5 us
    pallas_call x1, Pallas kernels, project(): pl.pallas_call(project_kernel, name='project', out_shape=(jax.ShapeDtypeS...  9.3 us

profile of v5, /device:TPU:0, one launch (start us, length us, event | category | flops | bytes accessed | tf_op | source)
XLA Modules:
  0.0 129.6 jit_solution(5226879085092827492)
XLA Ops:
  0.6 9.3 %project.1 = (bf16[128,1280]{1,0:T(8,128)(2,1)}, bf16[128,512]{1,0:T(8,128)(2,1)}) custom-call(bf16[20,128]{1,0:T(8,128)(2,1)} %bitcast.16, bf16[10,128]{1,0:T(8,128)(2,1)} %bitcast.18, bf16[2,128]{1,0:T(2,128)(2,1)} %bitcast.20, bf16[2,128]{1,0:T(2,128)(2,1)} %bitcast.21, s32[1,128]{1,0:T(1,128)} %bitcast.19, f32[1,128]{1,0:T(1,128)} %constant.2.clone.freq_hbm, ...), custom_call_target="tpu_custom_call" | custom-call | tf_op jit(solution)/shard_map/project/pallas_call | solution.py:141
  9.9 25.5 %attend.1 = (bf16[128,1280]{1,0:T(8,128)(2,1)}, bf16[128,512,128]{2,1,0:T(8,128)(2,1)}, bf16[128,512,128]{2,1,0:T(8,128)(2,1)}) custom-call(s32[128]{0:T(128)} %lens_ref.1, bf16[128,1280]{1,0:T(8,128)(2,1)} %get-tuple-element.8.q_hbm, bf16[128,512]{1,0:T(8,128)(2,1)} %get-tuple-element.9.kv_hbm, bf16[128,512,128]{2,1,0:T(8,128)(2,1)} %bitcast.14, ...), custom_call_target="tpu_custom_call" | custom-call | tf_op jit(solution)/shard_map/attend/pallas_call | solution.py:274
  35.5 91.7 %tail.1 = bf16[256,2560]{1,0:T(8,128)(2,1)} custom-call(bf16[20,128]{1,0:T(8,128)(2,1)} %bitcast.17, bf16[128,1280]{1,0:T(8,128)(2,1)} %get-tuple-element.10.attn_hbm, bf16[256,2560]{1,0:T(8,128)(2,1)} %x_hbm.3, bf16[1280,2560]{1,0:T(8,128)(2,1)} %wo_hbm.1, bf16[6848,2560]{1,0:T(8,128)(2,1)} %bitcast.12, bf16[6848,2560]{1,0:T(8,128)(2,1)} %bitcast.13, ...), custom_call_target="tpu_custom_call" | custom-call | tf_op jit(solution)/shard_map/tail/pallas_call | solution.py:720
  127.2 2.5 %copy.21 = bf16[256,2560]{1,0:T(8,128)(2,1)} copy(bf16[256,2560]{1,0:T(8,128)(2,1)} %tail.1) | data formatting | bytes 2621440

commit v6 on v5

--- a/solution.py
+++ b/solution.py
@@ -50,10 +50,11 @@
             source = wq_hbm.at[:, pl.ds(index * width, width)]
         else:
             source = (wk_hbm, wv_hbm)[index - q_chunks]
-        return pltpu.make_async_copy(source, w_buf.at[index], w_sems.at[index])
+        return pltpu.make_async_copy(source, w_buf.at[:, pl.ds(index * width, width)], w_sems.at[index])
 
     def weight_wait(index):
-        pltpu.make_async_copy(wk_hbm, w_buf.at[index], w_sems.at[index]).wait()
+        lanes = pl.ds(pl.multiple_of(index * width, width), width)
+        pltpu.make_async_copy(wk_hbm, w_buf.at[:, lanes], w_sems.at[index]).wait()
 
     smalls = [pltpu.make_async_copy(source, target, small_sems.at[slot]) for slot, (source, target) in enumerate((
         (lens_hbm, lens_ref), (freq_hbm, freq_ref), (gain_hbm, gain_ref), (bq_hbm, bq_ref), (bk_hbm, bk_ref), (bv_hbm, bv_ref)))]
@@ -105,15 +106,28 @@
     def part_copy(index):
         return remote(part_send.at[index], part_recv.at[index], index)
 
-    def multiply(index, carry):
-        weight_wait(index)
-        product = jnp.dot(normed[...], w_buf[index], preferred_element_type=F32)
-        part_own[index] = product[:half]
-        part_send[index] = product[half:].astype(BF16)
-        part_copy(index).start()
-        return carry
-
-    lax.fori_loop(0, chunks, multiply, 0)
+    def multiply(first, count):
+        for index in range(count):
+            weight_wait(first + index)
+        lanes = pl.ds(pl.multiple_of(first * width, width), count * width)
+        product = jnp.dot(normed[...], w_buf[:, lanes], preferred_element_type=F32)
+        for index in range(count):
+            value = product[:, index * width:(index + 1) * width]
+            part_own[first + index] = value[:half]
+            part_send[first + index] = value[half:].astype(BF16)
+        for index in range(count):
+            part_copy(first + index).start()
+
+    def multiply_pair(pair, carry):
+        multiply(2 * pair, 2)
+        return carry
+
+    def multiply_last(index, carry):
+        multiply(index, 1)
+        return carry
+
+    lax.fori_loop(0, chunks // 2, multiply_pair, 0)
+    lax.fori_loop(chunks - chunks % 2, chunks, multiply_last, 0)
     biases = [ref[...].astype(F32) for ref in (bq_ref, bk_ref, bv_ref)]
     for index in range(chunks):
         part_copy(index).wait()
@@ -154,7 +168,7 @@
             DMA((6,)),
             VMEM((rows, depth), BF16),
             DMA,
-            VMEM((chunks, depth, width), BF16),
+            VMEM((depth, chunks * width), BF16),
             VMEM((rows, depth), BF16),
             VMEM((rows, HEAD), F32),
             VMEM((rows, HEAD), F32),
@@ -194,13 +208,15 @@
     kv_copy = pltpu.make_async_copy(kv_hbm, kv_ref, small_sems.at[1])
     q_copy.start()
     kv_copy.start()
-    for step in range(3):
-        for kind in range(2):
-            load(step, kind).start()
+    for kind in range(2):
+        load(0, kind).start()
 
     q_wide[...] = jnp.zeros_like(q_wide)
     q_copy.wait()
     kv_copy.wait()
+    for step in range(1, 3):
+        for kind in range(2):
+            load(step, kind).start()
     for head in range(q_heads):
         q_wide[pl.ds(head, batch, stride=QPAD), :] = q_ref[:, head * HEAD:(head + 1) * HEAD].astype(F32)
     q_packed[...] = q_wide[...].astype(BF16)
@@ -303,9 +319,9 @@
 RING = 36
 
 
-def tail_kernel(gain_hbm, attn_hbm, x_hbm, wo_hbm, wg_hbm, wu_hbm, wd_hbm, out_hbm,
-                out_ref, gain_ref, gain_sem, pool, full, rows_in, part, keep, recv_one, send_two, recv_two, x_own, mid, sq_send, sq_recv,
-                h_rows, h_cols, gu_send, gu_recv, gu_own, act, early,
+def tail_kernel(gain_hbm, attn_hbm, x_hbm, wo_hbm, wg_hbm, wu_hbm, wd_hbm, out_ref,
+                gain_ref, gain_sem, pool, part, keep, recv_one, send_two, recv_two, x_own, mid, sq_send, sq_recv,
+                h_rows, h_cols, gu_send, gu_recv, gu_own, act,
                 pool_sems, x_sem, attn_sem, core_sems, rs_sems, ag_sems, gu_sems, act_sems):
     my = lax.axis_index("my")
     me = lax.axis_index("mx")
@@ -359,6 +375,8 @@
 
     own_half = pl.ds(pl.multiple_of(me * half, half), half)
     peer_half = pl.ds(pl.multiple_of(peer * half, half), half)
+    rows_in = h_rows.at[:, pl.ds(0, depth)]
+    full = h_rows.at[:, pl.ds(depth, depth)]
     attn_load = pltpu.make_async_copy(attn_hbm, full.at[own_half], attn_sem)
     attn_load.start()
     own_rows = pl.ds(pl.multiple_of(my * quarter, quarter), quarter)
@@ -625,8 +643,12 @@
     def pair_lanes(pair):
         return pl.ds(pl.multiple_of(pair * 2 * BLOCK, 2 * BLOCK), 2 * BLOCK)
 
+    early_slot = 3
+
     def down_early(pair, carry):
-        early[pair] = jnp.dot(act[:, late_lanes:], pool[late_row:, pair_lanes(pair)], preferred_element_type=F32)
+        value = jnp.dot(act[:, late_lanes:], pool[late_row:, pair_lanes(pair)], preferred_element_type=F32)
+        for piece in range(4):
+            gu_own[early_slot + 2 * pair + piece // 2, piece % 2] = value[:, piece * half:(piece + 1) * half]
         return carry
 
     lax.fori_loop(0, 1, down_early, 0)
@@ -653,9 +675,6 @@
         block = out_ref.at[owner_rows(first_side(chunk % 2)), columns(chunk)]
         return to_chip(block, block, second_side(chunk % 2), ag_sems.at[2, 0, chunk], ag_sems.at[2, 1, chunk])
 
-    def save_out(chunk):
-        return pltpu.make_async_copy(out_ref.at[:, columns(chunk)], out_hbm.at[:, columns(chunk)], pool_sems.at[chunk])
-
     def out_end(chunk):
         out_ref[owner_rows(my), columns(chunk)] = (mid[:, columns(chunk)] + scatter_end(chunk, chunk % 2)).astype(BF16)
         final_x(chunk).start()
@@ -667,7 +686,8 @@
 
     def down_rest(pair, carry):
         total = jnp.dot(act[:, :late_lanes], pool[down_slot * BLOCK:late_row, pair_lanes(pair)], preferred_element_type=F32)
-        scatter_start(pair, early[pair] + total)
+        pieces = [gu_own[early_slot + 2 * pair + piece // 2, piece % 2] for piece in range(4)]
+        scatter_start(pair, jnp.concatenate(pieces, axis=1) + total)
         return carry
 
     def down_pair(pair, carry):
@@ -703,12 +723,10 @@
     for chunk in range(col_chunks):
         (final_y if chunk % 2 == 0 else final_x)(chunk).wait_recv()
         final_cross(chunk).wait_recv()
-        save_out(chunk).start()
     for chunk in range(col_chunks):
         final_cross(chunk).wait_send()
         final_x(chunk).wait_send()
         final_y(chunk).wait_send()
-        save_out(chunk).wait()
 
 
 def tail(attn_rows, gain, x_in, w_o, wg_rows, wu_rows, w_down):
@@ -722,14 +740,11 @@
         name="tail",
         out_shape=jax.ShapeDtypeStruct((rows, hidden), BF16),
         in_specs=any_specs(7),
-        out_specs=any_specs(1)[0],
+        out_specs=vmem_specs(1)[0],
         scratch_shapes=[
-            VMEM((rows, hidden), BF16),
             VMEM((hidden // HEAD, HEAD), BF16),
             DMA,
             VMEM((RING * BLOCK, hidden), BF16),
-            VMEM((rows, depth), BF16),
-            VMEM((rows, depth), BF16),
             VMEM((chunks, 2 * quarter, BLOCK), BF16),
             VMEM((chunks, 2, quarter, BLOCK), F32),
             VMEM((chunks, 2 * quarter, BLOCK), BF16),
@@ -745,7 +760,6 @@
             VMEM((8, 2, BLOCK, half), BF16),
             VMEM((8, 2, BLOCK, half), F32),
             VMEM((rows, ff_chunks * BLOCK), BF16),
-            VMEM((2, rows, 2 * BLOCK), F32),
             DMA((RING,)),
             DMA,
             DMA,

time: 130 us -> 129 us (level)
  no operation moved by 1% of the time
where the time goes in v6:
time: 129 us
  Pallas kernels  126 us (98%)
  local copies, waits for them, and re-layouts  2.46 us (2%)
    pallas_call x1, Pallas kernels, tail(): pl.pallas_call(tail_kernel, name='tail', out_shape=jax.ShapeDtypeStruct((...  92.1 us
    pallas_call x1, Pallas kernels, attend(): pl.pallas_call(attend_kernel, name='attend', out_shape=(jax.ShapeDtypeStr...  25.2 us
    pallas_call x1, Pallas kernels, project(): pl.pallas_call(project_kernel, name='project', out_shape=(jax.ShapeDtypeS...  8.82 us

profile of v6, /device:TPU:0, one launch (start us, length us, event | category | flops | bytes accessed | tf_op | source)
XLA Modules:
  0.0 129.2 jit_solution(10516685328285684142)
XLA Ops:
  0.6 8.8 %project.1 = (bf16[128,1280]{1,0:T(8,128)(2,1)}, bf16[128,512]{1,0:T(8,128)(2,1)}) custom-call(bf16[20,128]{1,0:T(8,128)(2,1)} %bitcast.16, bf16[10,128]{1,0:T(8,128)(2,1)} %bitcast.18, bf16[2,128]{1,0:T(2,128)(2,1)} %bitcast.20, bf16[2,128]{1,0:T(2,128)(2,1)} %bitcast.21, s32[1,128]{1,0:T(1,128)} %bitcast.19, f32[1,128]{1,0:T(1,128)} %constant.2.clone.freq_hbm, ...), custom_call_target="tpu_custom_call" | custom-call | tf_op jit(solution)/shard_map/project/pallas_call | solution.py:155
  9.5 25.2 %attend.1 = (bf16[128,1280]{1,0:T(8,128)(2,1)}, bf16[128,512,128]{2,1,0:T(8,128)(2,1)}, bf16[128,512,128]{2,1,0:T(8,128)(2,1)}) custom-call(s32[128]{0:T(128)} %lens_ref.1, bf16[128,1280]{1,0:T(8,128)(2,1)} %get-tuple-element.8.q_hbm, bf16[128,512]{1,0:T(8,128)(2,1)} %get-tuple-element.9.kv_hbm, bf16[128,512,128]{2,1,0:T(8,128)(2,1)} %bitcast.14, ...), custom_call_target="tpu_custom_call" | custom-call | tf_op jit(solution)/shard_map/attend/pallas_call | solution.py:290
  34.7 92.1 %tail.1 = bf16[256,2560]{1,0:T(8,128)(2,1)} custom-call(bf16[20,128]{1,0:T(8,128)(2,1)} %bitcast.17, bf16[128,1280]{1,0:T(8,128)(2,1)} %get-tuple-element.10.attn_hbm, bf16[256,2560]{1,0:T(8,128)(2,1)} %x_hbm.3, bf16[1280,2560]{1,0:T(8,128)(2,1)} %wo_hbm.1, bf16[6848,2560]{1,0:T(8,128)(2,1)} %bitcast.12, bf16[6848,2560]{1,0:T(8,128)(2,1)} %bitcast.13, ...), custom_call_target="tpu_custom_call" | custom-call | tf_op jit(solution)/shard_map/tail/pallas_call | solution.py:738
  126.8 2.5 %copy.21 = bf16[256,2560]{1,0:T(8,128)(2,1)} copy(bf16[256,2560]{1,0:T(8,128)(2,1)} %tail.1) | data formatting | bytes 2621440

commit v7 on v6

--- a/solution.py
+++ b/solution.py
@@ -399,49 +399,59 @@
     for place, owner in enumerate((my, side_x, cross, side_y)):
         rows_in[place * quarter:(place + 1) * quarter, :] = full[pl.ds(pl.multiple_of(owner * quarter, quarter), quarter), :]
 
-    def columns(chunk):
-        if isinstance(chunk, int):
-            return slice(chunk * BLOCK, (chunk + 1) * BLOCK)
-        return pl.ds(pl.multiple_of(chunk * BLOCK, BLOCK), BLOCK)
+    sub = quarter // 2
+    wide = 2 * BLOCK
+    pairs = hidden // wide
+
+    def wide_cols(pair):
+        if isinstance(pair, int):
+            return slice(pair * wide, (pair + 1) * wide)
+        return pl.ds(pl.multiple_of(pair * wide, wide), wide)
 
     def first_side(parity):
-        return (side_x, side_y)[parity]
+        return side_x + parity * (side_y - side_x)
 
     def second_side(parity):
-        return (side_y, side_x)[parity]
+        return side_y + parity * (side_x - side_y)
+
+    def sub_rows(index):
+        if isinstance(index, int):
+            return slice(index * sub, (index + 1) * sub)
+        return pl.ds(pl.multiple_of(index * sub, sub), sub)
 
     def scatter_one(chunk, parity):
-        return to_chip(part.at[chunk], recv_one.at[chunk], first_side(parity), rs_sems.at[0, 0, chunk], rs_sems.at[0, 1, chunk])
+        lead = pl.ds(pl.multiple_of(sub * (1 + parity), sub), 2 * sub)
+        return to_chip(part.at[chunk, lead], recv_one.at[chunk], first_side(parity), rs_sems.at[0, 0, chunk], rs_sems.at[0, 1, chunk])
 
     def scatter_two(chunk, parity):
         return to_chip(send_two.at[chunk], recv_two.at[chunk], second_side(parity), rs_sems.at[1, 0, chunk], rs_sems.at[1, 1, chunk])
 
-    def scatter_start(pair, total):
-        for parity in range(2):
-            chunk = 2 * pair + parity
-            value = total[:, parity * BLOCK:(parity + 1) * BLOCK]
-            lead = quarter * (1 + parity)
-            part[chunk] = value[lead:lead + 2 * quarter].astype(BF16)
-            keep[chunk, 0] = value[:quarter]
-            other = 3 * quarter if parity == 0 else quarter
-            keep[chunk, 1] = value[other:other + quarter]
-        for parity in range(2):
-            scatter_one(2 * pair + parity, parity).start()
+    def scatter_store(pair, total):
+        for block in range(2):
+            chunk = 2 * pair + block
+            pieces = [total[place * quarter + block * sub:place * quarter + (block + 1) * sub] for place in range(4)]
+            for place in range(1, 4):
+                part[chunk, sub_rows(place), :] = pieces[place].astype(BF16)
+            keep[chunk, 0] = pieces[0]
+            keep[chunk, 1] = pieces[1]
+            keep[chunk, 2] = pieces[3]
 
     def scatter_pass(chunk, parity):
         scatter_one(chunk, parity).wait()
-        mine = slice(0, quarter) if parity == 0 else slice(quarter, 2 * quarter)
-        theirs = slice(quarter, 2 * quarter) if parity == 0 else slice(0, quarter)
-        send_two[chunk] = (keep[chunk, 1] + recv_one[chunk, theirs, :].astype(F32)).astype(BF16)
+        send_two[chunk] = (keep[chunk, 2 - parity] + recv_one[chunk, sub_rows(1 - parity), :].astype(F32)).astype(BF16)
         scatter_two(chunk, parity).start()
-        keep[chunk, 0] = keep[chunk, 0] + recv_one[chunk, mine, :].astype(F32)
+        keep[chunk, 0] = keep[chunk, 0] + recv_one[chunk, sub_rows(parity), :].astype(F32)
 
     def scatter_end(chunk, parity):
         scatter_two(chunk, parity).wait()
         return keep[chunk, 0] + recv_two[chunk].astype(F32)
 
-    def mid_end(chunk):
-        mid[:, columns(chunk)] = (x_own[:, columns(chunk)].astype(F32) + scatter_end(chunk, chunk % 2)).astype(BF16).astype(F32)
+    def turn(pair, block):
+        return (pair + block) % 2
+
+    def mid_end(pair, block):
+        before = x_own[sub_rows(block), wide_cols(pair)].astype(F32)
+        mid[sub_rows(block), wide_cols(pair)] = (before + scatter_end(2 * pair + block, turn(pair, block))).astype(BF16).astype(F32)
 
     x_copy.wait()
     gain_copy.wait()
@@ -451,65 +461,106 @@
         for copy in ff_copies(chunk):
             copy.start()
     def out_product(pair, carry):
-        lanes = pl.ds(pl.multiple_of(pair * 2 * BLOCK, 2 * BLOCK), 2 * BLOCK)
-        weights = pool[out_slot * BLOCK:out_slot * BLOCK + depth, lanes]
-        scatter_start(pair, jnp.dot(rows_in[...], weights, preferred_element_type=F32))
-        return carry
-
-    lax.fori_loop(0, col_chunks // 2, out_product, 0)
+        weights = pool[out_slot * BLOCK:out_slot * BLOCK + depth, wide_cols(pair)]
+        scatter_store(pair, jnp.dot(rows_in[...], weights, preferred_element_type=F32))
+        scatter_one(2 * pair, lax.rem(pair, 2)).start()
+        return carry
+
+    lax.fori_loop(0, pairs, out_product, 0)
+    gains = gain_ref[...].astype(F32)
+
+    def square_copy(block):
+        return to_core(sq_send.at[sub_rows(block)], sq_recv.at[sub_rows(block)], (core_sems.at[2 + 2 * block], core_sems.at[3 + 2 * block]))
+
+    def square_start(block):
+        square = jnp.zeros((sub, HEAD), F32)
+        for start in range(0, hidden, HEAD):
+            value = mid[sub_rows(block), start:start + HEAD]
+            square = square + value * value
+        sq_send[sub_rows(block), :] = jnp.broadcast_to(jnp.sum(square, axis=1, keepdims=True), (sub, HEAD))
+        square_copy(block).start()
+
+    def norm_rows(block):
+        square_copy(block).wait()
+        scale = lax.rsqrt((sq_send[sub_rows(block), :] + sq_recv[sub_rows(block), :]) / (2 * hidden) + NORM_EPS)
+        for start in range(0, hidden, HEAD):
+            gain = gains[start // HEAD:start // HEAD + 1, :]
+            h_rows[sub_rows(block), start:start + HEAD] = (mid[sub_rows(block), start:start + HEAD] * scale * gain).astype(BF16)
+
+    def h_block(place, pair, block):
+        return h_rows.at[sub_rows(2 * place + block), wide_cols(pair)]
+
+    def gather_x(pair, block):
+        chunk = 2 * pair + block
+        return to_chip(h_block(0, pair, block), h_block(1, pair, block), side_x, ag_sems.at[0, 0, chunk], ag_sems.at[0, 1, chunk])
+
+    def gather_y(pair, block):
+        chunk = 2 * pair + block
+        return to_chip(h_block(0, pair, block), h_block(3, pair, block), side_y, ag_sems.at[1, 0, chunk], ag_sems.at[1, 1, chunk])
+
+    def gather_cross(pair, block):
+        chunk = 2 * pair + block
+        source = 1 if turn(pair, block) == 0 else 3
+        return to_chip(h_block(source, pair, block), h_block(2, pair, block), second_side(turn(pair, block)),
+                       ag_sems.at[2, 0, chunk], ag_sems.at[2, 1, chunk])
+
+    def gather_send(pair, block):
+        gather_x(pair, block).start()
+        gather_y(pair, block).start()
+
+    def gather_pass(pair, block):
+        (gather_y if turn(pair, block) else gather_x)(pair, block).wait_recv()
+        gather_cross(pair, block).start()
+
+    def start_late(pair):
+        scatter_one(2 * pair + 1, turn(pair, 1)).start()
+
+    def pass_late(pair):
+        scatter_pass(2 * pair + 1, turn(pair, 1))
+
+    for pair in range(2):
+        start_late(pair)
     for chunk in range(out_slot // 2, chunk_ring):
         for copy in ff_copies(chunk):
             copy.start()
-    for chunk in range(col_chunks + 3):
-        if chunk < col_chunks:
-            scatter_pass(chunk, chunk % 2)
-        if chunk >= 3:
-            mid_end(chunk - 3)
-
-    square = jnp.zeros((quarter, HEAD), F32)
-    for start in range(0, hidden, HEAD):
-        square = square + mid[:, start:start + HEAD] * mid[:, start:start + HEAD]
-    sq_send[...] = jnp.broadcast_to(jnp.sum(square, axis=1, keepdims=True), (quarter, HEAD))
-    sq_copy = to_core(sq_send, sq_recv, (core_sems.at[2], core_sems.at[3]))
-    sq_copy.start()
-    sq_copy.wait()
-    scale = lax.rsqrt((sq_send[...] + sq_recv[...]) / (2 * hidden) + NORM_EPS)
-
-    def place_rows(place):
-        return slice(place * quarter, (place + 1) * quarter)
-
-    def gather_x(chunk):
-        return to_chip(h_rows.at[place_rows(0), columns(chunk)], h_rows.at[place_rows(1), columns(chunk)], side_x,
-                       ag_sems.at[0, 0, chunk], ag_sems.at[0, 1, chunk])
-
-    def gather_y(chunk):
-        return to_chip(h_rows.at[place_rows(0), columns(chunk)], h_rows.at[place_rows(3), columns(chunk)], side_y,
-                       ag_sems.at[1, 0, chunk], ag_sems.at[1, 1, chunk])
-
-    def gather_cross(chunk):
-        source = 1 if chunk % 2 == 0 else 3
-        return to_chip(h_rows.at[place_rows(source), columns(chunk)], h_rows.at[place_rows(2), columns(chunk)], second_side(chunk % 2),
-                       ag_sems.at[2, 0, chunk], ag_sems.at[2, 1, chunk])
-
-    gains = gain_ref[...].astype(F32)
-    for chunk in range(col_chunks):
-        for start in range(chunk * BLOCK, (chunk + 1) * BLOCK, HEAD):
-            gain = gains[start // HEAD:start // HEAD + 1, :]
-            h_rows[:quarter, start:start + HEAD] = (mid[:, start:start + HEAD] * scale * gain).astype(BF16)
-        gather_x(chunk).start()
-        gather_y(chunk).start()
-    for chunk in range(col_chunks):
-        (gather_x if chunk % 2 == 0 else gather_y)(chunk).wait_recv()
-        gather_cross(chunk).start()
-
-    for chunk in range(col_chunks):
-        (gather_y if chunk % 2 == 0 else gather_x)(chunk).wait_recv()
-        gather_cross(chunk).wait_recv()
+    for pair in range(pairs):
+        scatter_pass(2 * pair, turn(pair, 0))
+    for pair in range(2, pairs):
+        start_late(pair)
+    for pair in range(2):
+        pass_late(pair)
+    for pair in range(pairs):
+        mid_end(pair, 0)
+    square_start(0)
+    norm_rows(0)
+    for pair in range(2):
+        gather_send(pair, 0)
+    for pair in range(2, pairs):
+        pass_late(pair)
+    for pair in range(2, pairs):
+        gather_send(pair, 0)
+    for pair in range(pairs):
+        mid_end(pair, 1)
+    square_start(1)
+    for pair in range(2):
+        gather_pass(pair, 0)
+    norm_rows(1)
+    for pair in range(pairs):
+        gather_send(pair, 1)
+    for pair in range(2, pairs):
+        gather_pass(pair, 0)
+    for pair in range(pairs):
+        gather_pass(pair, 1)
+    for pair in range(pairs):
+        for block in range(2):
+            (gather_x if turn(pair, block) else gather_y)(pair, block).wait_recv()
+            gather_cross(pair, block).wait_recv()
         for place, source in enumerate((own_half, peer_half)):
-            h_cols[columns(chunk), place * half:(place + 1) * half] = h_rows[source, columns(chunk)].astype(F32).T.astype(BF16)
-        gather_x(chunk).wait_send()
-        gather_y(chunk).wait_send()
-        gather_cross(chunk).wait_send()
+            h_cols[wide_cols(pair), place * half:(place + 1) * half] = h_rows[source, wide_cols(pair)].astype(F32).T.astype(BF16)
+        for block in range(2):
+            gather_x(pair, block).wait_send()
+            gather_y(pair, block).wait_send()
+            gather_cross(pair, block).wait_send()
 
     def gu_copy(chunk):
         slot = lax.rem(chunk, 8)
@@ -640,13 +691,10 @@
     late_lanes = (ff_chunks - early_blocks) * BLOCK
     late_row = down_slot * BLOCK + late_lanes
 
-    def pair_lanes(pair):
-        return pl.ds(pl.multiple_of(pair * 2 * BLOCK, 2 * BLOCK), 2 * BLOCK)
-
     early_slot = 3
 
     def down_early(pair, carry):
-        value = jnp.dot(act[:, late_lanes:], pool[late_row:, pair_lanes(pair)], preferred_element_type=F32)
+        value = jnp.dot(act[:, late_lanes:], pool[late_row:, wide_cols(pair)], preferred_element_type=F32)
         for piece in range(4):
             gu_own[early_slot + 2 * pair + piece // 2, piece % 2] = value[:, piece * half:(piece + 1) * half]
         return carry
@@ -660,23 +708,26 @@
     for chunk in range(2 * ff_pairs - 6, ff_chunks):
         act_copy(chunk).wait()
 
-    def owner_rows(owner):
-        return pl.ds(pl.multiple_of(owner * quarter, quarter), quarter)
+    def out_block(owner, chunk):
+        pair, block = chunk // 2, chunk % 2
+        return out_ref.at[sub_rows(2 * owner + block), wide_cols(pair)]
 
     def final_x(chunk):
-        block = out_ref.at[owner_rows(my), columns(chunk)]
-        return to_chip(block, block, side_x, ag_sems.at[0, 0, chunk], ag_sems.at[0, 1, chunk])
+        target = out_block(my, chunk)
+        return to_chip(target, target, side_x, ag_sems.at[0, 0, chunk], ag_sems.at[0, 1, chunk])
 
     def final_y(chunk):
-        block = out_ref.at[owner_rows(my), columns(chunk)]
-        return to_chip(block, block, side_y, ag_sems.at[1, 0, chunk], ag_sems.at[1, 1, chunk])
+        target = out_block(my, chunk)
+        return to_chip(target, target, side_y, ag_sems.at[1, 0, chunk], ag_sems.at[1, 1, chunk])
 
     def final_cross(chunk):
-        block = out_ref.at[owner_rows(first_side(chunk % 2)), columns(chunk)]
-        return to_chip(block, block, second_side(chunk % 2), ag_sems.at[2, 0, chunk], ag_sems.at[2, 1, chunk])
+        target = out_block(first_side(chunk % 2), chunk)
+        return to_chip(target, target, second_side(chunk % 2), ag_sems.at[2, 0, chunk], ag_sems.at[2, 1, chunk])
 
     def out_end(chunk):
-        out_ref[owner_rows(my), columns(chunk)] = (mid[:, columns(chunk)] + scatter_end(chunk, chunk % 2)).astype(BF16)
+        pair, block = chunk // 2, chunk % 2
+        value = mid[sub_rows(block), wide_cols(pair)] + scatter_end(chunk, block)
+        out_ref[sub_rows(2 * my + block), wide_cols(pair)] = value.astype(BF16)
         final_x(chunk).start()
         final_y(chunk).start()
 
@@ -684,14 +735,19 @@
         (final_x if chunk % 2 == 0 else final_y)(chunk).wait_recv()
         final_cross(chunk).start()
 
+    def scatter_start(pair, total):
+        scatter_store(pair, total)
+        for block in range(2):
+            scatter_one(2 * pair + block, block).start()
+
     def down_rest(pair, carry):
-        total = jnp.dot(act[:, :late_lanes], pool[down_slot * BLOCK:late_row, pair_lanes(pair)], preferred_element_type=F32)
+        total = jnp.dot(act[:, :late_lanes], pool[down_slot * BLOCK:late_row, wide_cols(pair)], preferred_element_type=F32)
         pieces = [gu_own[early_slot + 2 * pair + piece // 2, piece % 2] for piece in range(4)]
         scatter_start(pair, jnp.concatenate(pieces, axis=1) + total)
         return carry
 
     def down_pair(pair, carry):
-        scatter_start(pair, jnp.dot(act[...], pool[down_slot * BLOCK:, pair_lanes(pair)], preferred_element_type=F32))
+        scatter_start(pair, jnp.dot(act[...], pool[down_slot * BLOCK:, wide_cols(pair)], preferred_element_type=F32))
 
         @pl.when(pair >= 2)
         def _():
@@ -699,7 +755,6 @@
                 scatter_pass(2 * (pair - 2) + parity, parity)
         return carry
 
-    pairs = col_chunks // 2
     lax.fori_loop(0, 2, down_rest, 0)
     lax.fori_loop(2, pairs, down_pair, 0)
 
@@ -745,11 +800,11 @@
             VMEM((hidden // HEAD, HEAD), BF16),
             DMA,
             VMEM((RING * BLOCK, hidden), BF16),
-            VMEM((chunks, 2 * quarter, BLOCK), BF16),
-            VMEM((chunks, 2, quarter, BLOCK), F32),
-            VMEM((chunks, 2 * quarter, BLOCK), BF16),
-            VMEM((chunks, quarter, BLOCK), BF16),
-            VMEM((chunks, quarter, BLOCK), BF16),
+            VMEM((chunks, 2 * quarter, 2 * BLOCK), BF16),
+            VMEM((chunks, 3, quarter // 2, 2 * BLOCK), F32),
+            VMEM((chunks, quarter, 2 * BLOCK), BF16),
+            VMEM((chunks, quarter // 2, 2 * BLOCK), BF16),
+            VMEM((chunks, quarter // 2, 2 * BLOCK), BF16),
             VMEM((quarter, hidden), BF16),
             VMEM((quarter, hidden), F32),
             VMEM((quarter, HEAD), F32),
@@ -763,7 +818,7 @@
             DMA((RING,)),
             DMA,
             DMA,
-            DMA((4,)),
+            DMA((6,)),
             DMA((2, 2, chunks)),
             DMA((3, 2, chunks)),
             DMA((2, 8)),

time: 129 us -> 126 us (0.977)
  Pallas kernels: 126 us -> 123 us
    pallas_call x1, Pallas kernels: 92.1 us -> 88.9 us  [tail(): pl.pallas_call(tail_kernel, name='tail', out_shape=jax.ShapeDtypeStruct((...]
where the time goes in v7:
time: 126 us
  Pallas kernels  123 us (98%)
  local copies, waits for them, and re-layouts  2.46 us (2%)
    pallas_call x1, Pallas kernels, tail(): pl.pallas_call(tail_kernel, name='tail', out_shape=jax.ShapeDtypeStruct((...  88.9 us
    pallas_call x1, Pallas kernels, attend(): pl.pallas_call(attend_kernel, name='attend', out_shape=(jax.ShapeDtypeStr...  25.2 us
    pallas_call x1, Pallas kernels, project(): pl.pallas_call(project_kernel, name='project', out_shape=(jax.ShapeDtypeS...  8.82 us

profile of v7, /device:TPU:0, one launch (start us, length us, event | category | flops | bytes accessed | tf_op | source)
XLA Modules:
  0.0 126.0 jit_solution(7750243366891012607)
XLA Ops:
  0.6 8.8 %project.1 = (bf16[128,1280]{1,0:T(8,128)(2,1)}, bf16[128,512]{1,0:T(8,128)(2,1)}) custom-call(bf16[20,128]{1,0:T(8,128)(2,1)} %bitcast.16, bf16[10,128]{1,0:T(8,128)(2,1)} %bitcast.18, bf16[2,128]{1,0:T(2,128)(2,1)} %bitcast.20, bf16[2,128]{1,0:T(2,128)(2,1)} %bitcast.21, s32[1,128]{1,0:T(1,128)} %bitcast.19, f32[1,128]{1,0:T(1,128)} %constant.2.clone.freq_hbm, ...), custom_call_target="tpu_custom_call" | custom-call | tf_op jit(solution)/shard_map/project/pallas_call | solution.py:155
  9.5 25.2 %attend.1 = (bf16[128,1280]{1,0:T(8,128)(2,1)}, bf16[128,512,128]{2,1,0:T(8,128)(2,1)}, bf16[128,512,128]{2,1,0:T(8,128)(2,1)}) custom-call(s32[128]{0:T(128)} %lens_ref.1, bf16[128,1280]{1,0:T(8,128)(2,1)} %get-tuple-element.8.q_hbm, bf16[128,512]{1,0:T(8,128)(2,1)} %get-tuple-element.9.kv_hbm, bf16[128,512,128]{2,1,0:T(8,128)(2,1)} %bitcast.14, ...), custom_call_target="tpu_custom_call" | custom-call | tf_op jit(solution)/shard_map/attend/pallas_call | solution.py:290
  34.7 88.9 %tail.1 = bf16[256,2560]{1,0:T(8,128)(2,1)} custom-call(bf16[20,128]{1,0:T(8,128)(2,1)} %bitcast.17, bf16[128,1280]{1,0:T(8,128)(2,1)} %get-tuple-element.10.attn_hbm, bf16[256,2560]{1,0:T(8,128)(2,1)} %x_hbm.3, bf16[1280,2560]{1,0:T(8,128)(2,1)} %wo_hbm.1, bf16[6848,2560]{1,0:T(8,128)(2,1)} %bitcast.12, bf16[6848,2560]{1,0:T(8,128)(2,1)} %bitcast.13, ...), custom_call_target="tpu_custom_call" | custom-call | tf_op jit(solution)/shard_map/tail/pallas_call | solution.py:793
  123.6 2.5 %copy.21 = bf16[256,2560]{1,0:T(8,128)(2,1)} copy(bf16[256,2560]{1,0:T(8,128)(2,1)} %tail.1) | data formatting | bytes 2621440

commit v8 on v7

--- a/solution.py
+++ b/solution.py
@@ -379,6 +379,8 @@
     full = h_rows.at[:, pl.ds(depth, depth)]
     attn_load = pltpu.make_async_copy(attn_hbm, full.at[own_half], attn_sem)
     attn_load.start()
+    for block in range(2):
+        out_copy(block).start()
     own_rows = pl.ds(pl.multiple_of(my * quarter, quarter), quarter)
     x_copy = pltpu.make_async_copy(x_hbm.at[own_rows], x_own, x_sem)
     x_copy.start()
@@ -390,7 +392,7 @@
     pl.semaphore_signal(barrier, inc=1, device_id={"my": side_x}, device_id_type=MESH)
     pl.semaphore_signal(barrier, inc=1, device_id={"my": side_y}, device_id_type=MESH)
     attn_load.wait()
-    for block in range(out_blocks):
+    for block in range(2, out_blocks):
         out_copy(block).start()
     pl.semaphore_wait(barrier, 3)
     attn_copy = to_core(full.at[own_half], full.at[own_half], (core_sems.at[0], core_sems.at[1]))
@@ -525,8 +527,8 @@
             copy.start()
     for pair in range(pairs):
         scatter_pass(2 * pair, turn(pair, 0))
-    for pair in range(2, pairs):
-        start_late(pair)
+        if 1 <= pair < pairs - 1:
+            start_late(pair + 1)
     for pair in range(2):
         pass_late(pair)
     for pair in range(pairs):
@@ -749,10 +751,10 @@
     def down_pair(pair, carry):
         scatter_start(pair, jnp.dot(act[...], pool[down_slot * BLOCK:, wide_cols(pair)], preferred_element_type=F32))
 
-        @pl.when(pair >= 2)
+        @pl.when(pair >= 3)
         def _():
             for parity in range(2):
-                scatter_pass(2 * (pair - 2) + parity, parity)
+                scatter_pass(2 * (pair - 3) + parity, parity)
         return carry
 
     lax.fori_loop(0, 2, down_rest, 0)
@@ -765,8 +767,7 @@
             else:
                 step(chunk)
 
-    each(out_end, 0)
-    for pair in range(pairs - 2, pairs):
+    for pair in range(pairs - 3, pairs):
         each(scatter_pass, pair)
         each(out_end, pair - pairs + 3)
     each(out_pass, 0)

time: 126 us -> 128 us (1.016)
    pallas_call x1, Pallas kernels: 88.9 us -> 90.3 us  [tail(): pl.pallas_call(tail_kernel, name='tail', out_shape=jax.ShapeDtypeStruct((...]
where the time goes in v8:
time: 128 us; the launch traced here: 127 us
  Pallas kernels  124 us (97%)
  local copies, waits for them, and re-layouts  2.46 us (2%)
    pallas_call x1, Pallas kernels, tail(): pl.pallas_call(tail_kernel, name='tail', out_shape=jax.ShapeDtypeStruct((...  90.3 us
    pallas_call x1, Pallas kernels, attend(): pl.pallas_call(attend_kernel, name='attend', out_shape=(jax.ShapeDtypeStr...  25.2 us
    pallas_call x1, Pallas kernels, project(): pl.pallas_call(project_kernel, name='project', out_shape=(jax.ShapeDtypeS...  8.82 us

profile of v8, /device:TPU:0, one launch (start us, length us, event | category | flops | bytes accessed | tf_op | source)
XLA Modules:
  0.0 127.4 jit_solution(12482700837622632870)
XLA Ops:
  0.6 8.8 %project.1 = (bf16[128,1280]{1,0:T(8,128)(2,1)}, bf16[128,512]{1,0:T(8,128)(2,1)}) custom-call(bf16[20,128]{1,0:T(8,128)(2,1)} %bitcast.16, bf16[10,128]{1,0:T(8,128)(2,1)} %bitcast.18, bf16[2,128]{1,0:T(2,128)(2,1)} %bitcast.20, bf16[2,128]{1,0:T(2,128)(2,1)} %bitcast.21, s32[1,128]{1,0:T(1,128)} %bitcast.19, f32[1,128]{1,0:T(1,128)} %constant.2.clone.freq_hbm, ...), custom_call_target="tpu_custom_call" | custom-call | tf_op jit(solution)/shard_map/project/pallas_call | solution.py:155
  9.5 25.2 %attend.1 = (bf16[128,1280]{1,0:T(8,128)(2,1)}, bf16[128,512,128]{2,1,0:T(8,128)(2,1)}, bf16[128,512,128]{2,1,0:T(8,128)(2,1)}) custom-call(s32[128]{0:T(128)} %lens_ref.1, bf16[128,1280]{1,0:T(8,128)(2,1)} %get-tuple-element.8.q_hbm, bf16[128,512]{1,0:T(8,128)(2,1)} %get-tuple-element.9.kv_hbm, bf16[128,512,128]{2,1,0:T(8,128)(2,1)} %bitcast.14, ...), custom_call_target="tpu_custom_call" | custom-call | tf_op jit(solution)/shard_map/attend/pallas_call | solution.py:290
  34.7 90.3 %tail.1 = bf16[256,2560]{1,0:T(8,128)(2,1)} custom-call(bf16[20,128]{1,0:T(8,128)(2,1)} %bitcast.17, bf16[128,1280]{1,0:T(8,128)(2,1)} %get-tuple-element.10.attn_hbm, bf16[256,2560]{1,0:T(8,128)(2,1)} %x_hbm.3, bf16[1280,2560]{1,0:T(8,128)(2,1)} %wo_hbm.1, bf16[6848,2560]{1,0:T(8,128)(2,1)} %bitcast.12, bf16[6848,2560]{1,0:T(8,128)(2,1)} %bitcast.13, ...), custom_call_target="tpu_custom_call" | custom-call | tf_op jit(solution)/shard_map/tail/pallas_call | solution.py:794
  125.0 2.5 %copy.21 = bf16[256,2560]{1,0:T(8,128)(2,1)} copy(bf16[256,2560]{1,0:T(8,128)(2,1)} %tail.1) | data formatting | bytes 2621440

commit v9 on v8

--- a/solution.py
+++ b/solution.py
@@ -527,19 +527,17 @@
             copy.start()
     for pair in range(pairs):
         scatter_pass(2 * pair, turn(pair, 0))
-        if 1 <= pair < pairs - 1:
-            start_late(pair + 1)
+    for pair in range(2, pairs):
+        start_late(pair)
     for pair in range(2):
         pass_late(pair)
     for pair in range(pairs):
         mid_end(pair, 0)
     square_start(0)
     norm_rows(0)
-    for pair in range(2):
-        gather_send(pair, 0)
     for pair in range(2, pairs):
         pass_late(pair)
-    for pair in range(2, pairs):
+    for pair in range(pairs):
         gather_send(pair, 0)
     for pair in range(pairs):
         mid_end(pair, 1)

time: 128 us -> 125 us (0.977)
  Pallas kernels: 124 us -> 122 us
    pallas_call x1, Pallas kernels: 90.3 us -> 87.6 us  [tail(): pl.pallas_call(tail_kernel, name='tail', out_shape=jax.ShapeDtypeStruct((...]
where the time goes in v9:
time: 125 us
  Pallas kernels  122 us (98%)
  local copies, waits for them, and re-layouts  2.46 us (2%)
    pallas_call x1, Pallas kernels, tail(): pl.pallas_call(tail_kernel, name='tail', out_shape=jax.ShapeDtypeStruct((...  87.6 us
    pallas_call x1, Pallas kernels, attend(): pl.pallas_call(attend_kernel, name='attend', out_shape=(jax.ShapeDtypeStr...  25.2 us
    pallas_call x1, Pallas kernels, project(): pl.pallas_call(project_kernel, name='project', out_shape=(jax.ShapeDtypeS...  8.82 us

profile of v9, /device:TPU:0, one launch (start us, length us, event | category | flops | bytes accessed | tf_op | source)
XLA Modules:
  0.0 124.7 jit_solution(1900051486843850799)
XLA Ops:
  0.6 8.8 %project.1 = (bf16[128,1280]{1,0:T(8,128)(2,1)}, bf16[128,512]{1,0:T(8,128)(2,1)}) custom-call(bf16[20,128]{1,0:T(8,128)(2,1)} %bitcast.16, bf16[10,128]{1,0:T(8,128)(2,1)} %bitcast.18, bf16[2,128]{1,0:T(2,128)(2,1)} %bitcast.20, bf16[2,128]{1,0:T(2,128)(2,1)} %bitcast.21, s32[1,128]{1,0:T(1,128)} %bitcast.19, f32[1,128]{1,0:T(1,128)} %constant.2.clone.freq_hbm, ...), custom_call_target="tpu_custom_call" | custom-call | tf_op jit(solution)/shard_map/project/pallas_call | solution.py:155
  9.5 25.2 %attend.1 = (bf16[128,1280]{1,0:T(8,128)(2,1)}, bf16[128,512,128]{2,1,0:T(8,128)(2,1)}, bf16[128,512,128]{2,1,0:T(8,128)(2,1)}) custom-call(s32[128]{0:T(128)} %lens_ref.1, bf16[128,1280]{1,0:T(8,128)(2,1)} %get-tuple-element.8.q_hbm, bf16[128,512]{1,0:T(8,128)(2,1)} %get-tuple-element.9.kv_hbm, bf16[128,512,128]{2,1,0:T(8,128)(2,1)} %bitcast.14, ...), custom_call_target="tpu_custom_call" | custom-call | tf_op jit(solution)/shard_map/attend/pallas_call | solution.py:290
  34.7 87.6 %tail.1 = bf16[256,2560]{1,0:T(8,128)(2,1)} custom-call(bf16[20,128]{1,0:T(8,128)(2,1)} %bitcast.17, bf16[128,1280]{1,0:T(8,128)(2,1)} %get-tuple-element.10.attn_hbm, bf16[256,2560]{1,0:T(8,128)(2,1)} %x_hbm.3, bf16[1280,2560]{1,0:T(8,128)(2,1)} %wo_hbm.1, bf16[6848,2560]{1,0:T(8,128)(2,1)} %bitcast.12, bf16[6848,2560]{1,0:T(8,128)(2,1)} %bitcast.13, ...), custom_call_target="tpu_custom_call" | custom-call | tf_op jit(solution)/shard_map/tail/pallas_call | solution.py:792
  122.3 2.5 %copy.21 = bf16[256,2560]{1,0:T(8,128)(2,1)} copy(bf16[256,2560]{1,0:T(8,128)(2,1)} %tail.1) | data formatting | bytes 2621440
